TPU v7x, 8 devices: a whole 2x2x1 slice. The times are simulated.
8 devices in a mesh: dp: 1 (over z), tx: 2 (over y), ty: 4 (over x, core).
Axes of the slice: x: 2, y: 2, z: 1, core: 2. Of those that a mesh axis runs over, the one named last changes fastest.
Arguments:
- x_in: bfloat16 [64, 256, 1536], P('dp', None, 'tx')
- ln1_gain: float32 [2, 1536], P(None, 'tx')
- ln1_bias: float32 [2, 1536], P(None, 'tx')
- w_q: bfloat16 [2, 1536, 16, 96], P(None, 'tx', 'ty')
- b_q: float32 [2, 16, 96], P(None, 'ty')
- w_k: bfloat16 [2, 1536, 16, 96], P(None, 'tx', 'ty')
- w_v: bfloat16 [2, 1536, 16, 96], P(None, 'tx', 'ty')
- b_v: float32 [2, 16, 96], P(None, 'ty')
- w_o: bfloat16 [2, 16, 96, 1536], P(None, 'ty', None, 'tx')
- b_o: float32 [2, 1536], P(None, 'tx')
- ln2_gain: float32 [2, 1536], P(None, 'tx')
- ln2_bias: float32 [2, 1536], P(None, 'tx')
- w_up: bfloat16 [2, 1536, 6144], P(None, 'tx', 'ty')
- b_up: float32 [2, 6144], P(None, 'ty')
- w_down: bfloat16 [2, 6144, 1536], P(None, 'ty', 'tx')
- b_down: float32 [2, 1536], P(None, 'tx')
Outputs:
- output: bfloat16 [64, 256, 1536], P('dp', None, 'tx')
All inputs are finite; a program needn't handle non-finite values.
Results may differ from a plain program's by a relative error of at most 0.02.
Values are sent between devices in bfloat16 or wider.
A program may use at most 1 GiB of HBM per device.

v0:
```python
import jax
import jax.numpy as jnp
from jax import lax
from jax.sharding import PartitionSpec as P

EPS = 1e-6


def split_norm(x_f, gain, shift, width):
    moments = lax.psum(jnp.stack([jnp.sum(x_f, axis=-1), jnp.sum(x_f * x_f, axis=-1)]), "tx")
    mean = (moments[0] / width)[..., None]
    variance = (moments[1] / width)[..., None] - mean * mean
    return ((x_f - mean) * lax.rsqrt(variance + EPS) * gain + shift).astype(jnp.bfloat16)


def solution(mesh):
    tx_size = mesh.shape["tx"]
    act_spec = P("dp", None, "tx")
    vec_tx = P(None, "tx")
    proj_spec = P(None, "tx", "ty", None)
    head_vec = P(None, "ty", None)
    in_specs = (act_spec, vec_tx, vec_tx, proj_spec, head_vec, proj_spec, proj_spec, head_vec,
                P(None, "ty", None, "tx"), vec_tx, vec_tx, vec_tx,
                P(None, "tx", "ty"), P(None, "ty"), P(None, "ty", "tx"), vec_tx)

    def local_fn(x_in, ln1_gain, ln1_bias, w_q, b_q, w_k, w_v, b_v, w_o, b_o, ln2_gain, ln2_bias, w_up, b_up, w_down, b_down):
        width = x_in.shape[-1] * tx_size
        scale = w_q.shape[-1] ** -0.5
        residual = x_in
        for layer in range(w_q.shape[0]):
            x_f = residual.astype(jnp.float32)
            normed = split_norm(x_f, ln1_gain[layer], ln1_bias[layer], width)
            part_q = jnp.einsum("bnw,whd->bnhd", normed, w_q[layer], preferred_element_type=jnp.float32).astype(jnp.bfloat16)
            part_k = jnp.einsum("bnw,whd->bnhd", normed, w_k[layer], preferred_element_type=jnp.float32).astype(jnp.bfloat16)
            part_v = jnp.einsum("bnw,whd->bnhd", normed, w_v[layer], preferred_element_type=jnp.float32).astype(jnp.bfloat16)
            sum_q, k_proj, sum_v = lax.psum((part_q, part_k, part_v), "tx")
            q_proj = (sum_q.astype(jnp.float32) + b_q[layer]).astype(jnp.bfloat16)
            v_proj = (sum_v.astype(jnp.float32) + b_v[layer]).astype(jnp.bfloat16)
            scores = jnp.einsum("bqhd,bkhd->bhqk", q_proj, k_proj, preferred_element_type=jnp.float32) * scale
            attn_prob = jax.nn.softmax(scores, axis=-1).astype(jnp.bfloat16)
            attended = jnp.einsum("bhqk,bkhd->bqhd", attn_prob, v_proj, preferred_element_type=jnp.float32).astype(jnp.bfloat16)
            part_o = jnp.einsum("bqhd,hdw->bqw", attended, w_o[layer], preferred_element_type=jnp.float32).astype(jnp.bfloat16)
            x_mid = (x_f + lax.psum(part_o, "ty").astype(jnp.float32) + b_o[layer]).astype(jnp.bfloat16)
            mid_f = x_mid.astype(jnp.float32)
            normed2 = split_norm(mid_f, ln2_gain[layer], ln2_bias[layer], width)
            part_up = jnp.einsum("bnw,wf->bnf", normed2, w_up[layer], preferred_element_type=jnp.float32).astype(jnp.bfloat16)
            hidden = jax.nn.gelu(lax.psum(part_up, "tx").astype(jnp.float32) + b_up[layer], approximate=True).astype(jnp.bfloat16)
            part_down = jnp.einsum("bnf,fw->bnw", hidden, w_down[layer], preferred_element_type=jnp.float32).astype(jnp.bfloat16)
            residual = (mid_f + lax.psum(part_down, "ty").astype(jnp.float32) + b_down[layer]).astype(jnp.bfloat16)
        return residual

    return jax.shard_map(local_fn, mesh=mesh, in_specs=in_specs, out_specs=act_spec, check_vma=False)
```

profile of v0, /device:TPU:0, one launch (start us, length us, event | category | flops | bytes accessed | tf_op | source)
XLA Modules:
  0.0 6392.4 jit_solution(563193542191149683)
XLA Ops:
  6.5 18.2 convert_reduce_fusion.3
  24.7 0.7 pad_maximum_fusion
  25.5 1.4 slice_reduce_fusion.6
  26.9 17.3 all-reduce.15.cloned.1.call-done
  44.2 0.9 fusion.130
  45.1 0.8 fusion.131
  45.9 22.3 convolution_convert_fusion.5
  68.2 15.2 convolution_convert_fusion.6
  83.4 15.2 convolution_convert_fusion.7
  100.4 820.2 %all-reduce.37.cloned.1.call-done = (bf16[64,256,4,96]{1,3,2,0:T(8,128)(2,1)}, bf16[64,256,4,96]{1,3,2,0:T(8,128)(2,1)}, bf16[64,256,4,96]{1,3,2,0:T(8,128)(2,1)}) async-done(((bf16[64,256,4,96]{1,3,2,0:T(8,128)(2,1)}, bf16[64,256,4,96]{1,3,2,0:T(8,128)(2,1)}, bf16[64,256,4,96]{1,3,2,0:T(8,128)(2,1)}), (bf16[64,256,4,96]{1,3,2,0:T(8,128)(2,1)}, bf16[64,256,4,96]{1,3,2,0:T(8,128)(2,1)}, ...) | async-done | bytes 37748752 | tf_op jit(solution)/shard_map/psum | solution.py:36
  920.6 31.0 fusion.78
  951.6 66.0 %fusion.151 = (f32[64,4,256]{2,1,0:T(4,128)S(1)}, f32[64,4,256,256]{2,3,1,0:T(8,128)}) fusion(f32[64,4,256,256]{2,3,1,0:T(8,128)} %fusion.78), kind=kOutput, calls=%fused_computation.198 | output fusion | flops 67109120 | bytes 134479872 | tf_op jit(solution)/shard_map/sub | solution.py:40
  1017.7 30.8 fusion.58
  1048.5 21.7 bitcast_convert_fusion.1
  1071.1 418.5 %all-reduce.17.cloned.1.call-done = bf16[64,256,768]{2,1,0:T(8,128)(2,1)} async-done(((bf16[64,256,768]{2,1,0:T(8,128)(2,1)}), bf16[64,256,768]{2,1,0:T(8,128)(2,1)}) %all-reduce.17.cloned.1.call-update) | async-done | bytes 25165840 | tf_op jit(solution)/shard_map/psum | solution.py:43
  1489.6 30.9 convert_reduce_fusion.2
  1520.5 0.7 pad_maximum_fusion.1
  1521.3 1.8 fusion.181
  1523.7 13.7 all-reduce.19.cloned.1.call-done
  1537.4 0.9 fusion.125
  1538.3 0.8 fusion.126
  1539.1 49.8 convolution_convert_fusion.1
  1590.2 1091.2 %all-reduce.21.cloned.1.call-done = bf16[64,256,1536]{2,1,0:T(8,128)(2,1)} async-done(((bf16[64,256,1536]{2,1,0:T(8,128)(2,1)}), bf16[64,256,1536]{2,1,0:T(8,128)(2,1)}) %all-reduce.21.cloned.1.call-update) | async-done | bytes 50331664 | tf_op jit(solution)/shard_map/psum | solution.py:47
  2681.4 75.0 %fusion.72 = bf16[64,256,768]{2,1,0:T(8,128)(2,1)} fusion(bf16[64,256,1536]{2,1,0:T(8,128)(2,1)} %all-reduce.21.cloned.1.call-done, f32[1536]{0:T(1024)S(1)} %get-tuple-element.14, bf16[2,1536,768]{2,1,0:T(8,128)(2,1)} %param.30), kind=kOutput, calls=%fused_computation.96 | convolution fusion | flops 38944112640 | bytes 77862912 | tf_op jit(solution)/shard_map/bnf,fw->bnw/dot_general | solution.py:48
  2757.2 418.9 %all-reduce.23.cloned.1.call-done = bf16[64,256,768]{2,1,0:T(8,128)(2,1)} async-done(((bf16[64,256,768]{2,1,0:T(8,128)(2,1)}), bf16[64,256,768]{2,1,0:T(8,128)(2,1)}) %all-reduce.23.cloned.1.call-update) | async-done | bytes 25165840 | tf_op jit(solution)/shard_map/psum | solution.py:49
  3176.0 30.9 convert_reduce_fusion.1
  3207.7 16.1 all-reduce.25.cloned.1.call-done
  3223.8 0.9 fusion.120
  3224.7 0.8 fusion.121
  3225.6 22.3 convolution_convert_fusion.2
  3247.9 15.3 convolution_convert_fusion.3
  3263.2 15.2 convolution_convert_fusion.4
  3278.5 821.8 %all-reduce.35.cloned.1.call-done = (bf16[64,256,4,96]{1,3,2,0:T(8,128)(2,1)}, bf16[64,256,4,96]{1,3,2,0:T(8,128)(2,1)}, bf16[64,256,4,96]{1,3,2,0:T(8,128)(2,1)}) async-done(((bf16[64,256,4,96]{1,3,2,0:T(8,128)(2,1)}, bf16[64,256,4,96]{1,3,2,0:T(8,128)(2,1)}, bf16[64,256,4,96]{1,3,2,0:T(8,128)(2,1)}), (bf16[64,256,4,96]{1,3,2,0:T(8,128)(2,1)}, bf16[64,256,4,96]{1,3,2,0:T(8,128)(2,1)}, ...) | async-done | bytes 37748752 | tf_op jit(solution)/shard_map/psum | solution.py:36
  4100.3 31.2 fusion.79
  4131.5 66.0 %fusion.152 = (f32[64,4,256]{2,1,0:T(4,128)S(1)}, f32[64,4,256,256]{2,3,1,0:T(8,128)}) fusion(f32[64,4,256,256]{2,3,1,0:T(8,128)} %fusion.79), kind=kOutput, calls=%fused_computation.199 | output fusion | flops 67109120 | bytes 134479872 | tf_op jit(solution)/shard_map/sub | solution.py:40
  4197.5 30.8 fusion.59
  4228.3 21.8 bitcast_convert_fusion
  4250.2 419.3 %all-reduce.27.cloned.1.call-done = bf16[64,256,768]{2,1,0:T(8,128)(2,1)} async-done(((bf16[64,256,768]{2,1,0:T(8,128)(2,1)}), bf16[64,256,768]{2,1,0:T(8,128)(2,1)}) %all-reduce.27.cloned.1.call-update) | async-done | bytes 25165840 | tf_op jit(solution)/shard_map/psum | solution.py:43
  4669.6 31.3 convert_reduce_fusion
  4701.6 1.8 fusion.179
  4703.5 14.3 all-reduce.29.cloned.1.call-done
  4717.8 0.9 fusion.115
  4718.7 0.8 fusion.116
  4719.5 49.8 convolution_convert_fusion
  4769.4 1092.4 %all-reduce.31.cloned.1.call-done = bf16[64,256,1536]{2,1,0:T(8,128)(2,1)} async-done(((bf16[64,256,1536]{2,1,0:T(8,128)(2,1)}), bf16[64,256,1536]{2,1,0:T(8,128)(2,1)}) %all-reduce.31.cloned.1.call-update) | async-done | bytes 50331664 | tf_op jit(solution)/shard_map/psum | solution.py:47
  5861.8 74.6 %fusion.75 = bf16[64,256,768]{2,1,0:T(8,128)(2,1)} fusion(bf16[64,256,1536]{2,1,0:T(8,128)(2,1)} %all-reduce.31.cloned.1.call-done, f32[1536]{0:T(1024)S(1)} %copy-done.6, bf16[2,1536,768]{2,1,0:T(8,128)(2,1)} %param.30), kind=kOutput, calls=%fused_computation.97 | convolution fusion | flops 38944112640 | bytes 77862912 | tf_op jit(solution)/shard_map/bnf,fw->bnw/dot_general | solution.py:48
  5936.5 419.5 %all-reduce.33.cloned.1.call-done = bf16[64,256,768]{2,1,0:T(8,128)(2,1)} async-done(((bf16[64,256,768]{2,1,0:T(8,128)(2,1)}), bf16[64,256,768]{2,1,0:T(8,128)(2,1)}) %all-reduce.33.cloned.1.call-update) | async-done | bytes 25165840 | tf_op jit(solution)/shard_map/psum | solution.py:49
  6356.0 29.4 fusion.47
  (72 shorter events, 6.9 us)
Async XLA Ops:
  6.5 37.6 all-reduce.15.cloned.1.call-start
  25.4 895.2 %all-reduce.37.cloned.1.call-start = ((), (), s32[]{:S(2)}) async-start(), calls=%async_computation.11 | async-start | bytes 75497472 | tf_op jit(solution)/shard_map/psum | solution.py:36
  45.9 22.3 copy-start
  83.4 15.8 copy-start.15
  83.4 16.4 copy-start.16
  98.7 1390.9 %all-reduce.17.cloned.1.call-start = ((), (), s32[]{:S(2)}) async-start(), calls=%async_computation.1 | async-start | bytes 50331648 | tf_op jit(solution)/shard_map/psum | solution.py:43
  1017.6 30.8 copy-start.18
  1048.5 22.0 copy-start.7
  1070.2 452.9 %copy-start.8 = (f32[2,768]{1,0:T(2,128)S(1)}, f32[2,768]{1,0:T(2,128)}, u32[]{:S(2)}) copy-start(f32[2,768]{1,0:T(2,128)} %param.27) | copy-start | bytes 18436
  1070.2 452.9 %copy-start.9 = (f32[2,768]{1,0:T(2,128)S(1)}, f32[2,768]{1,0:T(2,128)}, u32[]{:S(2)}) copy-start(f32[2,768]{1,0:T(2,128)} %param.26) | copy-start | bytes 18436
  1070.2 467.2 %all-reduce.19.cloned.1.call-start = ((), (), s32[]{:S(2)}) async-start(), calls=%async_computation.2 | async-start | bytes 262144 | tf_op jit(solution)/shard_map/psum | solution.py:10
  1521.2 1160.2 %all-reduce.21.cloned.1.call-start = ((), (), s32[]{:S(2)}) async-start(), calls=%async_computation.3 | async-start | bytes 100663296 | tf_op jit(solution)/shard_map/psum | solution.py:47
  1588.9 0.7 copy-start.5
  1588.9 1587.1 %all-reduce.23.cloned.1.call-start = ((), (), s32[]{:S(2)}) async-start(), calls=%async_computation.4 | async-start | bytes 50331648 | tf_op jit(solution)/shard_map/psum | solution.py:49
  2681.4 75.2 %copy-start.10 = (f32[2,768]{1,0:T(2,128)S(1)}, f32[2,768]{1,0:T(2,128)}, u32[]{:S(2)}) copy-start(f32[2,768]{1,0:T(2,128)} %param.31) | copy-start | bytes 18436
  2756.5 469.1 %copy-start.11 = (f32[768]{0:T(1024)S(1)}, f32[768]{0:T(1024)}, u32[]{:S(2)}) copy-start(f32[768]{0:T(1024)} %get-tuple-element.25) | copy-start | bytes 9220
  2756.5 469.1 %copy-start.12 = (f32[768]{0:T(1024)S(1)}, f32[768]{0:T(1024)}, u32[]{:S(2)}) copy-start(f32[768]{0:T(1024)} %get-tuple-element.45) | copy-start | bytes 9220
  2756.5 467.3 %all-reduce.25.cloned.1.call-start = ((), (), s32[]{:S(2)}) async-start(), calls=%async_computation.5 | async-start | bytes 262144 | tf_op jit(solution)/shard_map/psum | solution.py:10
  3207.6 892.6 %all-reduce.35.cloned.1.call-start = ((), (), s32[]{:S(2)}) async-start(), calls=%async_computation.10 | async-start | bytes 75497472 | tf_op jit(solution)/shard_map/psum | solution.py:36
  3225.6 22.3 copy-start.1
  3263.2 837.1 %copy-start.2 = (f32[4,96]{1,0:T(4,128)S(1)}, f32[4,96]{1,0:T(4,128)}, u32[]{:S(2)}) copy-start(f32[4,96]{1,0:T(4,128)} %get-tuple-element.38) | copy-start | bytes 4612
  3278.4 1391.2 %all-reduce.27.cloned.1.call-start = ((), (), s32[]{:S(2)}) async-start(), calls=%async_computation.6 | async-start | bytes 50331648 | tf_op jit(solution)/shard_map/psum | solution.py:43
  4131.5 66.0 %copy-start.17 = (f32[4,96]{1,0:T(4,128)S(1)}, f32[4,96]{1,0:T(4,128)}, u32[]{:S(2)}) copy-start(f32[4,96]{1,0:T(4,128)} %get-tuple-element.36) | copy-start | bytes 4612
  4197.5 30.9 copy-start.19
  4228.3 441.2 %copy-start.3 = (f32[768]{0:T(1024)S(1)}, f32[768]{0:T(1024)}, u32[]{:S(2)}) copy-start(f32[768]{0:T(1024)} %get-tuple-element.21) | copy-start | bytes 9220
  4250.2 469.3 %copy-start.13 = (f32[768]{0:T(1024)S(1)}, f32[768]{0:T(1024)}, u32[]{:S(2)}) copy-start(f32[768]{0:T(1024)} %get-tuple-element.19) | copy-start | bytes 9220
  4250.2 469.3 %copy-start.14 = (f32[768]{0:T(1024)S(1)}, f32[768]{0:T(1024)}, u32[]{:S(2)}) copy-start(f32[768]{0:T(1024)} %get-tuple-element.47) | copy-start | bytes 9220
  4250.2 467.6 %all-reduce.29.cloned.1.call-start = ((), (), s32[]{:S(2)}) async-start(), calls=%async_computation.7 | async-start | bytes 262144 | tf_op jit(solution)/shard_map/psum | solution.py:10
  4701.6 1160.2 %all-reduce.31.cloned.1.call-start = ((), (), s32[]{:S(2)}) async-start(), calls=%async_computation.8 | async-start | bytes 100663296 | tf_op jit(solution)/shard_map/psum | solution.py:47
  4769.3 1092.5 %copy-start.6 = (f32[1536]{0:T(1024)S(1)}, f32[1536]{0:T(1024)}, u32[]{:S(2)}) copy-start(f32[1536]{0:T(1024)} %get-tuple-element.13) | copy-start | bytes 18436
  4769.3 1586.6 %all-reduce.33.cloned.1.call-start = ((), (), s32[]{:S(2)}) async-start(), calls=%async_computation.9 | async-start | bytes 50331648 | tf_op jit(solution)/shard_map/psum | solution.py:49
  5861.8 494.2 %copy-start.4 = (f32[768]{0:T(1024)S(1)}, f32[768]{0:T(1024)}, u32[]{:S(2)}) copy-start(f32[768]{0:T(1024)} %get-tuple-element.15) | copy-start | bytes 9220
Sparse Core Ops, SparseCore 0:
  25.5 18.5 all-reduce.14
  98.8 821.7 all-reduce.36
  1070.3 419.2 all-reduce.16
  1521.3 16.0 all-reduce.18
  1589.1 1092.3 all-reduce.20
  2756.6 419.3 all-reduce.22
  3207.8 16.0 all-reduce.24
  3278.5 821.7 all-reduce.34
  4250.3 419.2 all-reduce.26
  4701.7 16.0 all-reduce.28
  4769.5 1092.3 all-reduce.30
  5936.6 419.3 all-reduce.32
where the time goes:
time: 6400 us; the launch traced here: 6390 us
  waiting for transfers between devices  5560 us (87%)
  matrix products  522 us (8%)
  other arithmetic  282 us (4%)
    psum x2, waiting for transfers between devices, local_fn(): lax.psum(part_up, 'tx').astype(jnp.float32) + b_up[layer]  2180 us
    psum x2, waiting for transfers between devices, local_fn(): sum_q, k_proj, sum_v = lax.psum((part_q, part_k, part_v), 'tx')  1640 us
    psum x2, waiting for transfers between devices, local_fn(): lax.psum(part_down, 'ty').astype(jnp.float32)  838 us
    psum x2, waiting for transfers between devices, local_fn(): lax.psum(part_o, 'ty').astype(jnp.float32)  838 us
    dot_general x2, matrix products, local_fn(): jnp.einsum('bnf,fw->bnw', hidden, w_down[layer], preferred_element_type=j...  150 us
    sub x2, other arithmetic, local_fn(): attn_prob = jax.nn.softmax(scores, axis=-1).astype(jnp.bfloat16)  132 us
  transfers between devices with their start and end apart: 12, of which 12 were waited for; matrix products, arithmetic and copies ran while one was open for 0% of the time, Pallas kernels for 0%

commit v1 on v0

v1 whole, which is shorter than its diff:
```python
import math

import jax
import jax.numpy as jnp
from jax import lax
from jax.experimental import pallas as pl
from jax.experimental.pallas import tpu as pltpu
from jax.sharding import PartitionSpec as P

EPS = 1e-6
F32 = jnp.float32
BF16 = jnp.bfloat16
MESH = pl.DeviceIdType.MESH

IMGS = 8
NTOK = 256
TILES = 4
TT = 512
HD = 96
GH = 4
GF = GH * HD
HW = 768
FB = 1536
UC = 384
DC = 256
NA, NU, ND = 4, 4, 3
PER_LAYER = NA + NU + ND
LAYERS = 2
CHUNKS = LAYERS * PER_LAYER
UNITS = ND * TILES

X, Y, C = 2, 4, 1
XC, YC, XY, XYC = 3, 5, 6, 7

NN = (((1,), (0,)), ((), ()))
NT = (((1,), (1,)), ((), ()))
TN = (((0,), (0,)), ((), ()))


def dot(a, b, dims=NN):
    return lax.dot_general(a, b, dims, preferred_element_type=F32)


def gelu(x):
    return 0.5 * x * (1.0 + jnp.tanh(x * (0.7978845608028654 + 0.035677408136300125 * (x * x))))


def chunk_kind(k):
    layer, j = divmod(k, PER_LAYER)
    if j < NA:
        return layer, "a", j
    if j < NA + NU:
        return layer, "u", j - NA
    return layer, "d", j - NA - NU


def relay_on_x(k):
    layer, kind, j = chunk_kind(k)
    return (layer, kind) in ((0, "a"), (0, "u"), (1, "a"))


LINK = 45.5e3
LOOK = 3
T_ATT, T_UP, T_DOWN = 6.0, 3.3, 4.3


def chunk_bytes(k):
    return 2 * (FB * DC if chunk_kind(k)[1] == "d" else GF * HW)


def plan():
    free = {"x": 0.0, "y": 0.0, "c": 0.0}
    ready = {}
    pending = []
    program = []
    now = [0.0]

    def send(link, size, lag=2.5):
        rate = 450e3 if link == "c" else LINK
        start = max(free[link], now[0])
        free[link] = start + size / rate
        return free[link] + lag

    def arrive(name, time, action=None, rank=1):
        ready[name] = time
        if action is not None:
            pending.append((time, rank, action))

    def do(action):
        program.append(("do", action))
        kind = action[0]
        if kind == "ownx":
            arrive(("w", X, action[1]), send("x", chunk_bytes(action[1])), ("gotx", action[1]), 2)
        elif kind == "owny":
            arrive(("w", Y, action[1]), send("y", chunk_bytes(action[1])), ("goty", action[1]))
        elif kind == "ownc":
            arrive(("w", C, action[1]), send("c", chunk_bytes(action[1])))
        elif kind == "image":
            arrive(("image", action[1]), send("y", NTOK * HW * 2))
        elif kind == "gotx":
            k = action[1]
            arrive(("w", XC, k), send("c", chunk_bytes(k)))
            if not relay_on_x(k):
                arrive(("w", XY, k), send("y", chunk_bytes(k)), ("gotd", k))
            if k >= LOOK and k + LOOK < CHUNKS:
                do(("ownx", k + LOOK))
            if k == LOOK - 1:
                for j in range(LOOK, 2 * LOOK):
                    do(("ownx", j))
        elif kind == "goty":
            k = action[1]
            arrive(("w", YC, k), send("c", chunk_bytes(k)))
            if relay_on_x(k):
                arrive(("w", XY, k), send("x", chunk_bytes(k)), ("gotd", k))
            if k + LOOK < CHUNKS:
                do(("owny", k + LOOK))
                do(("ownc", k + LOOK))
        elif kind == "gotd":
            arrive(("w", XYC, action[1]), send("c", chunk_bytes(action[1])))
        elif kind == "out":
            size = TT * DC * 2
            q = action[1]
            arrive(("o", X, q), send("x", size), ("outx", q), 2)
            arrive(("o", Y, q), send("y", size), ("outy", q))
            arrive(("o", C, q), send("c", size))
        elif kind == "outx":
            arrive(("o", XC, action[1]), send("c", TT * DC * 2))
        elif kind == "outy":
            arrive(("o", XY, action[1]), send("x", TT * DC * 2), ("outd", action[1]))
            arrive(("o", YC, action[1]), send("c", TT * DC * 2))
        elif kind == "outd":
            arrive(("o", XYC, action[1]), send("c", TT * DC * 2))

    def pump():
        while True:
            due = [p for p in pending if p[0] <= now[0]]
            if not due:
                return
            first = min(due, key=lambda p: (p[0], p[1]))
            pending.remove(first)
            do(first[2])

    def block(layer, kind, n, needs, cost):
        while True:
            pump()
            late = [ready.get(a, 1e9) for a in needs if ready.get(a, 1e9) > now[0]]
            if not late and all(a in ready for a in needs):
                break
            times = [p[0] for p in pending] + [t for t in late if t < 1e9]
            now[0] = max(now[0], min(times))
        program.append(("block", layer, kind, n))
        now[0] += cost

    do(("small",))
    for k in range(LOOK):
        do(("ownx", k))
        do(("owny", k))
        do(("ownc", k))
    for i in range(IMGS):
        do(("image", i))

    def whole(k):
        return [("w", s, k) for s in (X, Y, C, XC, YC, XY, XYC)]

    for layer in range(LAYERS):
        base = layer * PER_LAYER
        for n in range(4 * TILES):
            needs = [a for k in range(NA - 1) for a in whole(base + k)]
            if n % 4 == 3:
                needs += whole(base + NA - 1)
            if layer == 0:
                needs += [("image", i) for i in range(2 * (n // 4) + 2)]
            block(layer, "a", n, needs, T_ATT)
        for n in range(NU * TILES):
            block(layer, "u", n, whole(base + NA + n // TILES), T_UP)
        for n in range(ND * TILES):
            block(layer, "d", n, whole(base + NA + NU + n // TILES), T_DOWN)
            if layer == LAYERS - 1 and n >= 1:
                do(("out", n - 1))
    do(("out", UNITS - 1))
    while pending:
        now[0] = max(now[0], min(p[0] for p in pending))
        pump()
    return program, max(now[0], max(ready.values()))


def mega_kernel(x_in, wq, wk, wv, wo, wup, wdown, vec_own, hid_own,
                y_out, land_a, land_u, land_d,
                x0, x1, h, u, ubuf, dbuf, vec_oth, hid,
                wsend, wrecv, isend, irecv, osend, orecv, small_send, small_recv,
                local_sem, asem, usem, dsem):
    ty, tx = lax.axis_index("ty"), lax.axis_index("tx")
    core, xx = lax.rem(ty, 2), ty // 2
    me = tx * 4 + ty
    over_x = {"ty": (1 - xx) * 2 + core}
    over_y = {"tx": 1 - tx}
    over_c = {"ty": xx * 2 + (1 - core)}
    place = {X: tx * 4 + (1 - xx) * 2 + core, Y: (1 - tx) * 4 + ty, XY: (1 - tx) * 4 + (1 - xx) * 2 + core, 0: me}
    other = {s: p + 1 - 2 * core for s, p in place.items()}
    place.update({s + 1: p for s, p in other.items()})
    src_wa = (wq, wk, wv, wo)

    barrier = pltpu.get_barrier_semaphore()
    for peer in (over_x, over_y, over_c):
        pl.semaphore_signal(barrier, inc=1, device_id=peer, device_id_type=MESH)
    pl.semaphore_wait(barrier, 3)

    def remote(src, dst, send, recv, peer):
        return pltpu.make_async_remote_copy(src_ref=src, dst_ref=dst, send_sem=send, recv_sem=recv,
                                            device_id=peer, device_id_type=MESH)

    def own_ref(k):
        layer, kind, j = chunk_kind(k)
        if kind == "a":
            return src_wa[j].at[layer]
        if kind == "u":
            return wup.at[layer, :, j * UC:(j + 1) * UC]
        return wdown.at[layer, :, j * DC:(j + 1) * DC]

    def land_ref(k, s):
        layer, kind, j = chunk_kind(k)
        if kind == "a":
            return land_a.at[layer, s - 1, j * GF:(j + 1) * GF, :]
        if kind == "u":
            return land_u.at[layer, s - 1, :, j * UC:(j + 1) * UC]
        return land_d.at[layer, s - 1, :, j * DC:(j + 1) * DC]

    def weight_copy(k, s):
        if s == X:
            src, peer = own_ref(k), over_x
        elif s == Y:
            src, peer = own_ref(k), over_y
        elif s == C:
            src, peer = own_ref(k), over_c
        elif s == XY:
            src, peer = (land_ref(k, Y), over_x) if relay_on_x(k) else (land_ref(k, X), over_y)
        else:
            src, peer = land_ref(k, s - 1), over_c
        return remote(src, land_ref(k, s), wsend.at[k, s - 1], wrecv.at[k, s - 1], peer)

    def image_copy(i):
        theirs = (1 - tx) * 4 + ty
        return remote(x_in.at[theirs * IMGS + i], x1.at[i], isend.at[i], irecv.at[i], over_y)

    def out_ref(slot, q):
        cc, i = divmod(q, TILES)
        return y_out.at[pl.ds(place[slot] * IMGS + 2 * i, 2), :, cc * DC:(cc + 1) * DC]

    def out_copy(q, s):
        cc, i = divmod(q, TILES)
        cols = slice(cc * DC, (cc + 1) * DC)
        rows = slice(2 * i, 2 * i + 2)
        if s == X:
            src, dst, peer = x0.at[rows, :, cols], out_ref(0, q), over_x
        elif s == C:
            src, dst, peer = x0.at[rows, :, cols], out_ref(0, q), over_c
        elif s == Y:
            src, dst, peer = x1.at[rows, :, cols], out_ref(0, q), over_y
        elif s == XY:
            src, dst, peer = out_ref(Y, q), out_ref(Y, q), over_x
        else:
            src, dst, peer = out_ref(s - 1, q), out_ref(s - 1, q), over_c
        return remote(src, dst, osend.at[q, s - 1], orecv.at[q, s - 1], peer)

    def keep_copy(q):
        cc, i = divmod(q, TILES)
        return pltpu.make_async_copy(x0.at[2 * i:2 * i + 2, :, cc * DC:(cc + 1) * DC], out_ref(0, q), dsem.at[2, q])

    def out_arrived(q, s):
        return remote(out_ref(s, q), out_ref(s, q), osend.at[q, s - 1], orecv.at[q, s - 1], over_x)

    vec_copy = remote(vec_own, vec_oth, small_send.at[0], small_recv.at[0], over_y)
    hid_x = remote(hid_own, hid.at[X], small_send.at[1], small_recv.at[1], over_x)
    hid_c = remote(hid_own, hid.at[C], small_send.at[2], small_recv.at[2], over_c)
    hid_xc = remote(hid.at[X], hid.at[XC], small_send.at[3], small_recv.at[3], over_c)
    own_rows = pltpu.make_async_copy(x_in.at[pl.ds(me * IMGS, IMGS)], x0, local_sem.at[0])
    own_hid = pltpu.make_async_copy(hid_own, hid.at[0], local_sem.at[1])

    def act(action):
        kind, *k = action
        k = k[0] if k else None
        if kind == "small":
            vec_copy.start()
            hid_x.start()
            hid_c.start()
            own_rows.start()
            own_hid.start()
        elif kind == "ownx":
            weight_copy(k, X).start()
        elif kind == "owny":
            weight_copy(k, Y).start()
        elif kind == "ownc":
            weight_copy(k, C).start()
        elif kind == "image":
            image_copy(k).start()
        elif kind == "gotx":
            weight_copy(k, X).wait_recv()
            if not relay_on_x(k):
                weight_copy(k, XY).start()
            weight_copy(k, XC).start()
        elif kind == "goty":
            weight_copy(k, Y).wait_recv()
            if relay_on_x(k):
                weight_copy(k, XY).start()
            weight_copy(k, YC).start()
        elif kind == "gotd":
            weight_copy(k, XY).wait_recv()
            weight_copy(k, XYC).start()
        elif kind == "out":
            for s in (X, Y, C):
                out_copy(k, s).start()
            keep_copy(k).start()
        elif kind == "outx":
            out_arrived(k, X).wait_recv()
            out_copy(k, XC).start()
        elif kind == "outy":
            out_arrived(k, Y).wait_recv()
            out_copy(k, XY).start()
            out_copy(k, YC).start()
        elif kind == "outd":
            out_arrived(k, XY).wait_recv()
            out_copy(k, XYC).start()

    def slot_ref(land, own, layer, s):
        return own.at[layer] if s == 0 else land.at[layer, s - 1]

    def a_loads(layer, r):
        out = []
        for dy in range(2):
            s = dy * 4 + r
            cols = slice(r * 2 * HW + dy * HW, r * 2 * HW + (dy + 1) * HW)
            if s == 0:
                for j in range(3):
                    out.append((src_wa[j].at[layer], u.at[j * GF:(j + 1) * GF, cols], asem.at[s, j]))
            else:
                out.append((land_a.at[layer, s - 1, 0:3 * GF, :], u.at[0:3 * GF, cols], asem.at[s, 0]))
        return [pltpu.make_async_copy(*c) for c in out]

    def o_loads(layer):
        out = []
        for r in range(4):
            for dy in range(2):
                s = dy * 4 + r
                src = wo.at[layer] if s == 0 else land_a.at[layer, s - 1, 3 * GF:4 * GF, :]
                at = 3 * GF + (r % 2) * GF
                cols = slice((r // 2) * 2 * HW + dy * HW, (r // 2) * 2 * HW + (dy + 1) * HW)
                out.append(pltpu.make_async_copy(src, u.at[at:at + GF, cols], asem.at[s, 3]))
        return out

    def u_loads(layer, k):
        b = k % 2
        out = []
        for r in range(4):
            for dy in range(2):
                s = dy * 4 + r
                src = slot_ref(land_u, wup, layer, s).at[:, k * UC:(k + 1) * UC]
                out.append(pltpu.make_async_copy(
                    src, ubuf.at[b, dy * HW:(dy + 1) * HW, r * UC:(r + 1) * UC], usem.at[b, s]))
        return out

    def d_loads(layer, cc):
        b = cc % 2
        out = []
        for r in range(4):
            for dy in range(2):
                s = dy * 4 + r
                src = slot_ref(land_d, wdown, layer, s).at[:, cc * DC:(cc + 1) * DC]
                out.append(pltpu.make_async_copy(
                    src, dbuf.at[b, r * FB:(r + 1) * FB, dy * DC:(dy + 1) * DC], dsem.at[b, s]))
        return out

    def start(copies):
        for c in copies:
            c.start()

    def finish(copies):
        for c in copies:
            c.wait()

    def arrived(k):
        for s in (C, XC, YC, XYC):
            weight_copy(k, s).wait_recv()

    def vec_row(layer, j):
        at = slice(layer * 6 + j, layer * 6 + j + 1)
        return vec_own[at, :], vec_oth[at, :]

    def norm(layer, j, tile):
        g0, g1 = vec_row(layer, j)
        s0, s1 = vec_row(layer, j + 1)
        rows = 64

        @pl.loop(0, TT // rows)
        def _(i):
            img = 2 * tile + i // (NTOK // rows)
            at = pl.ds(pl.multiple_of(lax.rem(i, NTOK // rows) * rows, rows), rows)
            a = x0[img, at, :].astype(F32)
            b = x1[img, at, :].astype(F32)
            width = 2.0 * HW
            mean = (jnp.sum(a, 1, keepdims=True) + jnp.sum(b, 1, keepdims=True)) / width
            a = a - mean
            b = b - mean
            var = (jnp.sum(a * a, 1, keepdims=True) + jnp.sum(b * b, 1, keepdims=True)) / width
            inv = lax.rsqrt(var + EPS)
            to = pl.ds(pl.multiple_of(tile * TT + i * rows, rows), rows)
            h[to, :HW] = (a * inv * g0 + s0).astype(BF16)
            h[to, HW:] = (b * inv * g1 + s1).astype(BF16)

    scale = HD ** -0.5 * math.log2(math.e)
    qkv = dbuf.at[0, 4 * GF:7 * GF, :]
    ot = dbuf.at[0, 0:4 * GF, :]

    def column(layer, r, at):
        row = hid[r, layer:layer + 1, at:at + GF]
        col = jnp.broadcast_to(row, (128, GF)).T
        return jnp.concatenate([col] * (TT // 128), 1)

    def attention_block(layer, tile, r):
        rows = pl.ds(pl.multiple_of(tile * TT, TT), TT)
        cols = pl.ds(pl.multiple_of(r * 2 * HW, 2 * HW), 2 * HW)
        hh = h[rows, :]
        qkv[0:GF, :] = (dot(u[0:GF, cols], hh, NT) + column(layer, r, 0)).astype(BF16)
        qkv[GF:2 * GF, :] = dot(u[GF:2 * GF, cols], hh, NT).astype(BF16)
        qkv[2 * GF:3 * GF, :] = (dot(u[2 * GF:3 * GF, cols], hh, NT) + column(layer, r, GF)).astype(BF16)
        for img in range(TT // NTOK):
            c = slice(img * NTOK, (img + 1) * NTOK)
            for hd in range(GH):
                qt = qkv[hd * HD:(hd + 1) * HD, c]
                kt = qkv[GF + hd * HD:GF + (hd + 1) * HD, c]
                vt = qkv[2 * GF + hd * HD:2 * GF + (hd + 1) * HD, c]
                st = dot(kt, qt, TN)
                top = jnp.max(st, 0, keepdims=True)
                e = jnp.exp2((st - top) * scale)
                p = (e * (1.0 / jnp.sum(e, 0, keepdims=True))).astype(BF16)
                ot[pl.ds(pl.multiple_of(r * GF, GF) + hd * HD, HD), c] = dot(vt, p).astype(BF16)

    def project_block(layer, tile):
        b0, b1 = vec_row(layer, 2)
        o = ot[...].T
        imgs = pl.ds(2 * tile, 2)
        for half, ref, bias in ((0, x0, b0), (1, x1, b1)):
            acc = dot(o[:, :HW], u[3 * GF:5 * GF, half * HW:(half + 1) * HW])
            acc += dot(o[:, HW:], u[3 * GF:5 * GF, 2 * HW + half * HW:2 * HW + (half + 1) * HW])
            old = ref[imgs].reshape(TT, HW).astype(F32)
            ref[imgs] = (old + acc + bias).astype(BF16).reshape(2, NTOK, HW)

    def up_block(layer, k, tile, b):
        rows = pl.ds(pl.multiple_of(tile * TT, TT), TT)
        for nb in range(2):
            bias = jnp.concatenate(
                [hid[2 * nb + j, layer:layer + 1, pl.ds(pl.multiple_of(2 * GF + k * UC, 128), UC)] for j in range(2)], 1)
            t = gelu(dot(h[rows, :], ubuf[b, :, nb * 2 * UC:(nb + 1) * 2 * UC]) + bias).astype(BF16)
            for j in range(2):
                u[rows, pl.ds(pl.multiple_of((2 * nb + j) * FB + k * UC, 128), UC)] = t[:, j * UC:(j + 1) * UC]

    def down_block(layer, cc, tile, b):
        rows = pl.ds(pl.multiple_of(tile * TT, TT), TT)
        imgs = pl.ds(2 * tile, 2)
        cols = pl.ds(pl.multiple_of(cc * DC, DC), DC)
        at = layer * 6 + 5
        acc = dot(u[rows, :], dbuf[b])
        for half, ref, vec in ((0, x0, vec_own), (1, x1, vec_oth)):
            old = ref[imgs, :, cols].reshape(TT, DC).astype(F32)
            new = old + acc[:, half * DC:(half + 1) * DC] + vec[at:at + 1, cols]
            ref[imgs, :, cols] = new.astype(BF16).reshape(2, NTOK, DC)

    program, _ = plan()
    before = {}
    todo = []
    tail = []
    for item in program:
        if item[0] == "do":
            todo.append(item[1])
        else:
            before[item[1:]] = todo
            todo = []
    tail = todo

    def ahead(layer, kind, n, count):
        for m in range(count):
            actions = before[(layer, kind, m)]
            if actions and not (layer == 0 and kind == "a" and m == 0):
                @pl.when(n == m)
                def _(actions=actions):
                    for a in actions:
                        act(a)

    for a in before[(0, "a", 0)]:
        act(a)
    hid_x.wait_recv()
    hid_xc.start()
    hid_c.wait_recv()
    hid_xc.wait_recv()
    vec_copy.wait_recv()
    own_rows.wait()
    own_hid.wait()

    for layer in range(LAYERS):
        base = layer * PER_LAYER

        @pl.loop(0, 4 * TILES)
        def _(n, layer=layer, base=base):
            ahead(layer, "a", n, 4 * TILES)
            tile, r = n // 4, lax.rem(n, 4)

            @pl.when(n == 0)
            def _():
                for k in range(NA - 1):
                    arrived(base + k)
                for q in range(4):
                    start(a_loads(layer, q))

            @pl.when(n == 3)
            def _():
                arrived(base + NA - 1)
                start(o_loads(layer))

            for q in range(4):
                @pl.when(n == q)
                def _(q=q):
                    finish(a_loads(layer, q))

            @pl.when(r == 0)
            def _():
                if layer == 0:
                    for i in range(TILES):
                        @pl.when(tile == i)
                        def _(i=i):
                            image_copy(2 * i).wait_recv()
                            image_copy(2 * i + 1).wait_recv()
                norm(layer, 0, tile)
            attention_block(layer, tile, r)

            @pl.when(n == 3)
            def _():
                finish(o_loads(layer))

            @pl.when(r == 3)
            def _():
                project_block(layer, tile)
                norm(layer, 3, tile)

        @pl.loop(0, NU * TILES)
        def _(n, layer=layer, base=base):
            ahead(layer, "u", n, NU * TILES)
            k, tile = n // TILES, lax.rem(n, TILES)
            b = lax.rem(k, 2)
            for j in range(NU):
                @pl.when(n == j * TILES)
                def _(j=j):
                    arrived(base + NA + j)
                    start(u_loads(layer, j))
                    finish(u_loads(layer, j))
            up_block(layer, k, tile, b)

        @pl.loop(0, ND * TILES)
        def _(n, layer=layer, base=base):
            ahead(layer, "d", n, ND * TILES)
            cc, tile = n // TILES, lax.rem(n, TILES)
            b = lax.rem(cc, 2)
            for j in range(ND):
                @pl.when(n == j * TILES)
                def _(j=j):
                    arrived(base + NA + NU + j)
                    start(d_loads(layer, j))
                    finish(d_loads(layer, j))
            down_block(layer, cc, tile, b)

    for a in tail:
        act(a)
    for q in range(UNITS):
        keep_copy(q).wait()
        for s in (C, XC, YC, XYC):
            out_arrived(q, s).wait_recv()
        for s in range(1, 8):
            out_copy(q, s).wait_send()
    for k in range(CHUNKS):
        for s in range(1, 8):
            weight_copy(k, s).wait_send()
    for i in range(IMGS):
        image_copy(i).wait_send()
    for c in (vec_copy, hid_x, hid_c, hid_xc):
        c.wait_send()


def mega(x_in, wq, wk, wv, wo, wup, wdown, vec, hid):
    any_spec = pl.BlockSpec(memory_space=pl.ANY)
    vm = pl.BlockSpec(memory_space=pltpu.VMEM)
    dma = pltpu.SemaphoreType.DMA
    shapes = (x_in.shape, (LAYERS, 7, 4 * GF, HW), (LAYERS, 7, HW, FB), (LAYERS, 7, FB, HW))
    flops = 2 * 2048 * 1536 * 16384 * LAYERS
    return pl.pallas_call(
        mega_kernel,
        out_shape=tuple(jax.ShapeDtypeStruct(s, BF16) for s in shapes),
        in_specs=[any_spec] * 7 + [vm] * 2,
        out_specs=[any_spec] * 4,
        scratch_shapes=[
            pltpu.VMEM((IMGS, NTOK, HW), BF16), pltpu.VMEM((IMGS, NTOK, HW), BF16),
            pltpu.VMEM((IMGS * NTOK, 2 * HW), BF16), pltpu.VMEM((IMGS * NTOK, 4 * FB), BF16),
            pltpu.VMEM((2, 2 * HW, 4 * UC), BF16), pltpu.VMEM((2, 4 * FB, 2 * DC), BF16),
            pltpu.VMEM(vec.shape, F32), pltpu.VMEM((4,) + hid.shape, F32),
            dma((CHUNKS, 7)), dma((CHUNKS, 7)), dma((IMGS,)), dma((IMGS,)), dma((UNITS, 7)), dma((UNITS, 7)),
            dma((4,)), dma((4,)), dma((2,)), dma((8, 4)), dma((2, 8)), dma((3, UNITS)),
        ],
        compiler_params=pltpu.CompilerParams(collective_id=0, has_side_effects=True, vmem_limit_bytes=67043328),
        cost_estimate=pl.CostEstimate(flops=flops, bytes_accessed=300 << 20, transcendentals=0),
        name="encoder",
    )(x_in, wq, wk, wv, wo, wup, wdown, vec, hid)[0]


def solution(mesh):
    act_spec = P("dp", None, "tx")
    vec_tx = P(None, "tx")
    proj_spec = P(None, "tx", "ty", None)
    head_vec = P(None, "ty", None)
    in_specs = (act_spec, vec_tx, vec_tx, proj_spec, head_vec, proj_spec, proj_spec, head_vec,
                P(None, "ty", None, "tx"), vec_tx, vec_tx, vec_tx,
                P(None, "tx", "ty"), P(None, "ty"), P(None, "ty", "tx"), vec_tx)

    def heads_first(w):
        return jnp.transpose(w, (0, 2, 3, 1)).reshape(LAYERS, GF, HW)

    def local_fn(x_in, ln1_gain, ln1_bias, w_q, b_q, w_k, w_v, b_v, w_o, b_o, ln2_gain, ln2_bias, w_up, b_up, w_down, b_down):
        vec = jnp.stack([ln1_gain, ln1_bias, b_o, ln2_gain, ln2_bias, b_down], 1).reshape(6 * LAYERS, HW)
        vec = jnp.pad(vec, ((0, 16 - 6 * LAYERS), (0, 0)))
        hid = jnp.concatenate([b_q.reshape(LAYERS, GF), b_v.reshape(LAYERS, GF), b_up], -1)
        hid = jnp.pad(hid, ((0, 8 - LAYERS), (0, 0)))
        return mega(x_in, heads_first(w_q), heads_first(w_k), heads_first(w_v), w_o.reshape(LAYERS, GF, HW),
                    w_up, w_down, vec, hid)

    return jax.shard_map(local_fn, mesh=mesh, in_specs=in_specs, out_specs=act_spec, check_vma=False)
```

time: 6400 us -> 736 us (0.12)
  waiting for transfers between devices: 5560 us -> 0 us
  Pallas kernels: 0 us -> 707 us
  matrix products: 522 us -> 0 us
  other arithmetic: 282 us -> 1.35 us
    psum x12 -> x0, waiting for transfers between devices: 5560 us -> none  [the longest x2 2180 us: local_fn(): lax.psum(part_up, 'tx').astype(jnp.float32) + b_up[layer]]
    pallas_call x0 -> x1, Pallas kernels: none -> 707 us  [mega(): pl.pallas_call(mega_kernel, out_shape=tuple((jax.ShapeDtypeStruct(s, BF16...]
    dot_general x16 -> x0, matrix products: 522 us -> none  [the longest x2 150 us: local_fn(): jnp.einsum('bnf,fw->bnw', hidden, w_down[layer], preferred_element_type=j...]
    sub x2 -> x0, other arithmetic: 132 us -> none  [local_fn(): attn_prob = jax.nn.softmax(scores, axis=-1).astype(jnp.bfloat16)]
    reduce_sum x4 -> x0, other arithmetic: 111 us -> none  [split_norm(): jnp.sum(x_f, axis=-1)]
  transfers between devices with their start and end apart: 12 -> 0, of which waited for: 12 -> 0; matrix products, arithmetic and copies ran while one was open for 0% -> 0% of each run, Pallas kernels for 0% -> 0%
where the time goes in v1:
time: 736 us; the launch traced here: 735 us
  Pallas kernels  707 us (96%)
  local copies, waits for them, and re-layouts  27.1 us (4%)
    pallas_call x1, Pallas kernels, mega(): pl.pallas_call(mega_kernel, out_shape=tuple((jax.ShapeDtypeStruct(s, BF16...  707 us
    unnamed x6, local copies, waits for them, and re-layouts  24.2 us

profile of v1, /device:TPU:0, one launch (start us, length us, event | category | flops | bytes accessed | tf_op | source)
XLA Modules:
  0.0 735.2 jit_solution(13094895067449168112)
XLA Ops:
  0.0 0.8 reshape.26
  0.8 0.8 reshape.27
  1.5 0.7 constant_dynamic-update-slice_fusion.5
  2.2 0.7 constant_dynamic-update-slice_fusion.4
  2.9 0.7 constant_dynamic-update-slice_fusion.3
  3.6 0.7 constant_dynamic-update-slice_fusion.2
  4.3 0.7 constant_dynamic-update-slice_fusion.1
  5.0 0.7 constant_dynamic-update-slice_fusion
  5.7 0.6 pad.8.vec_own
  6.4 1.4 select_maximum_fusion.hid_own
  7.7 706.7 %encoder.1 = (bf16[64,256,768]{2,1,0:T(8,128)(2,1)}, bf16[2,7,1536,768]{3,2,1,0:T(8,128)(2,1)}, bf16[2,7,768,1536]{3,2,1,0:T(8,128)(2,1)}, bf16[2,7,1536,768]{3,2,1,0:T(8,128)(2,1)}) custom-call(bf16[64,256,768]{2,1,0:T(8,128)(2,1)} %x_in.1, bf16[2,384,768]{2,1,0:T(8,128)(2,1)} %bitcast.22, bf16[2,384,768]{2,1,0:T(8,128)(2,1)} %bitcast.23, ...), custom_call_target="tpu_custom_call" | custom-call | flops 206158430208 | bytes 314572800 | tf_op jit(solution)/shard_map/encoder/pallas_call | solution.py:592
  714.5 20.7 %copy.25 = bf16[64,256,768]{2,1,0:T(8,128)(2,1)} copy(bf16[64,256,768]{2,1,0:T(8,128)(2,1)} %get-tuple-element.6) | data formatting | bytes 50331648
  (2 shorter events, 0.0 us)

commit v2 on v1

v2 whole, which is shorter than its diff:
```python
import math

import jax
import jax.numpy as jnp
from jax import lax
from jax.experimental import pallas as pl
from jax.experimental.pallas import tpu as pltpu
from jax.sharding import PartitionSpec as P

EPS = 1e-6
F32 = jnp.float32
BF16 = jnp.bfloat16
MESH = pl.DeviceIdType.MESH

IMGS = 8
NTOK = 256
TOKENS = IMGS * NTOK
TILES = 4
TT = 512
HD = 96
GH = 4
GF = GH * HD
HW = 768
FB = 1536
UC = 384
DC = 128
NA, NU = 4, 4
ND = 6
DB = 2
PER_LAYER = NA + NU + ND
LAYERS = 2
CHUNKS = LAYERS * PER_LAYER
UNITS = ND * TILES
NB = 768
VR = HD + 16

X, Y, C = 2, 4, 1
XC, YC, XY, XYC = 3, 5, 6, 7

NN = (((1,), (0,)), ((), ()))
NT = (((1,), (1,)), ((), ()))
TN = (((0,), (0,)), ((), ()))


def dot(a, b, dims=NN):
    return lax.dot_general(a, b, dims, preferred_element_type=F32)


def gelu(x):
    return 0.5 * x * (1.0 + jnp.tanh(x * (0.7978845608028654 + 0.035677408136300125 * (x * x))))


def chunk_kind(k):
    layer, j = divmod(k, PER_LAYER)
    if j < NA:
        return layer, "a", j
    if j < NA + NU:
        return layer, "u", j - NA
    return layer, "d", j - NA - NU


LINK = 46.6e3
BACKLOG = 12.0
MODES = "xxxxxyxxyxxxyxxyyyyxyxyyyyyy"
RANK_X = "fhihkapyflvgprzumqtwuwsxzzzu"
RANK_Y = "hlbjoqorrtnphopfjmmonfkjiljh"
RANK_R = "cxtlosbypmfyjtepgfjseseimaah"
RANK_I = "coboceni"
EARLY, OUTS = 17, 2
BLOCKS = {"a": 16, "p": TILES, "u": NU * TILES, "d": ND * TILES}


def behind(letter):
    return 5 * (ord(letter) - ord("m"))


def relay_on_x(k):
    return MODES[k] == "x"


def chunk_bytes(k):
    return 2 * (FB * DC if chunk_kind(k)[1] == "d" else GF * HW)


def block_cost(kind, n):
    if kind == "a":
        return 3.06 + (1.25 if n < 4 else 0.0)
    return {"p": 3.87, "u": 3.16, "d": 46.0 / (ND * TILES)}[kind]


def plan():
    free = {"x": 0.0, "y": 0.0, "c": 0.0}
    ready = {}
    pending = []
    program = []
    now = [4.5]
    queue = {"x": [(10 * k + behind(RANK_X[k]), ("ownx", k)) for k in range(CHUNKS)],
             "y": [(10 * k + behind(RANK_Y[k]), ("owny", k)) for k in range(CHUNKS)]
             + [(20 + 3 * i + behind(RANK_I[i]), ("image", i)) for i in range(IMGS)]}
    given = set()
    passed = {None}
    unit = TT * DC * 2

    def send(link, size):
        rate, lag = (450e3, 1.5) if link == "c" else (LINK, 2.5)
        free[link] = max(free[link], now[0]) + size / rate
        return free[link] + lag

    def arrive(name, time, action=None):
        ready[name] = time
        if action is not None:
            pending.append((time, action))

    loads = []
    for layer in range(LAYERS):
        base = layer * PER_LAYER
        old = (layer - 1, "d", BLOCKS["d"] - 1) if layer else None
        for r in range(4):
            loads.append((("la", layer, r), [("w", s, base + j) for s in (r, 4 + r) if s for j in range(3)], old, 1.9))
        loads.append((("lo", layer), [("w", s, base + 3) for s in range(1, 8)], old, 2.2))
        for k in range(NU):
            last = (layer, "u", (k - 2) * TILES + TILES - 1) if k > 1 else old and (layer - 1, "u", BLOCKS["u"] - 1)
            loads.append((("lu", layer, k), [("w", s, base + NA + k) for s in range(1, 8)], last, 2.2))
        for j in range(ND):
            last = (layer, "d", (j - DB) * TILES + TILES - 1) if j >= DB else (layer, "p", TILES - 1)
            loads.append((("ld", layer, j), [("w", s, base + NA + NU + j) for s in range(1, 8)], last, 1.8))

    def do(action):
        program.append(("do", action))
        kind, *k = action
        k = k[0] if k else None
        if kind == "ownx":
            arrive(("w", X, k), send("x", chunk_bytes(k)), ("gotx", k))
        elif kind == "owny":
            arrive(("w", Y, k), send("y", chunk_bytes(k)), ("goty", k))
        elif kind == "ownc":
            arrive(("w", C, k), send("c", chunk_bytes(k)))
        elif kind == "image":
            arrive(("image", k), send("y", NTOK * HW * 2))
        elif kind == "gotx":
            arrive(("w", XC, k), send("c", chunk_bytes(k)))
            if not relay_on_x(k):
                queue["y"].append((10 * k + behind(RANK_R[k]), ("relay", k)))
        elif kind == "goty":
            arrive(("w", YC, k), send("c", chunk_bytes(k)))
            if relay_on_x(k):
                queue["x"].append((10 * k + behind(RANK_R[k]), ("relay", k)))
        elif kind == "relay":
            arrive(("w", XY, k), send("x" if relay_on_x(k) else "y", chunk_bytes(k)), ("gotd", k))
        elif kind == "gotd":
            arrive(("w", XYC, k), send("c", chunk_bytes(k)))
        elif kind == "out":
            queue["y"].append((10 * CHUNKS - EARLY + OUTS * k, ("outp", k)))
            arrive(("o", X, k), send("x", unit), ("outx", k))
            arrive(("o", C, k), send("c", unit))
        elif kind == "outp":
            arrive(("o", Y, k), send("y", unit), ("outy", k))
        elif kind == "outx":
            arrive(("o", XC, k), send("c", unit))
        elif kind == "outy":
            arrive(("o", XY, k), send("x", unit), ("outd", k))
            arrive(("o", YC, k), send("c", unit))
        elif kind == "outd":
            arrive(("o", XYC, k), send("c", unit))

    def pump():
        while True:
            due = [p for p in pending if p[0] <= now[0]]
            if due:
                first = min(due)
                pending.remove(first)
                do(first[1])
                continue
            for link in ("y", "x"):
                if queue[link] and free[link] - now[0] < BACKLOG:
                    first = min(queue[link])
                    queue[link].remove(first)
                    do(first[1])
                    if first[1][0] in ("ownx", "owny") and first[1][1] not in given:
                        given.add(first[1][1])
                        do(("ownc", first[1][1]))
                    break
            else:
                break
        for load in list(loads):
            action, needs, last, cost = load
            if last in passed and all(ready.get(a, 1e9) <= now[0] for a in needs):
                loads.remove(load)
                program.append(("do", action))
                ready[action] = now[0] + cost

    def block(layer, kind, n, needs, cost):
        while True:
            pump()
            late = [ready.get(a, 1e9) for a in needs if ready.get(a, 1e9) > now[0]]
            if not late:
                break
            times = [p[0] for p in pending] + [t for t in ready.values() if t > now[0]]
            times += [free[link] - BACKLOG + 1e-6 for link in queue if queue[link]]
            now[0] = max(now[0], min(times))
        program.append(("block", layer, kind, n))
        passed.add((layer, kind, n))
        now[0] += cost

    mark = []
    do(("small",))
    pump()
    for layer in range(LAYERS):
        for n in range(BLOCKS["a"]):
            needs = [("la", layer, n // 4)]
            if layer == 0 and n < 4:
                needs += [("image", 2 * n), ("image", 2 * n + 1)]
            block(layer, "a", n, needs, block_cost("a", n))
        for n in range(TILES):
            block(layer, "p", n, [("lo", layer)], block_cost("p", n))
        for n in range(BLOCKS["u"]):
            block(layer, "u", n, [("lu", layer, n // TILES)], block_cost("u", n))
        for n in range(BLOCKS["d"]):
            if layer == LAYERS - 1 and n == 0:
                do(("leave",))
            block(layer, "d", n, [("ld", layer, n // TILES)], block_cost("d", n))
            mark.append(now[0])
            if layer == LAYERS - 1 and n >= 1:
                do(("out", n - 1))
    do(("out", UNITS - 1))
    while pending or queue["y"]:
        times = [p[0] for p in pending] + [free["y"] - BACKLOG + 1e-6 for _ in queue["y"]]
        now[0] = max(now[0], min(times))
        pump()
    return program, max(now[0], max(ready.values())), mark


def mega_kernel(x_in, wq, wk, wv, wo, wup, wdown, *rest):
    vec_own, hid_own, rest = rest[:6], rest[6:9], rest[9:]
    big, land_a, land_u, land_d, x1, u, dbuf, qkv = rest[:8]
    vec_oth, hid, rest = rest[8:14], rest[14:17], rest[17:]
    encoder_body(x_in, wq, wk, wv, wo, wup, wdown, vec_own, hid_own, big, land_a, land_u, land_d,
                 x1, u, dbuf, qkv, vec_oth, hid, *rest)


def encoder_body(x_in, wq, wk, wv, wo, wup, wdown, vec_own, hid_own, big, land_a, land_u, land_d,
                 x1, u, dbuf, qkv, vec_oth, hid,
                wsend, wrecv, isend, irecv, osend, orecv, small_send, small_recv,
                local_sem, asem, usem, dsem, credit):
    ty, tx = lax.axis_index("ty"), lax.axis_index("tx")
    core, xx = lax.rem(ty, 2), ty // 2
    me = tx * 4 + ty
    x0 = big.at[0:TOKENS, 0:HW]
    h = big.at[TOKENS:2 * TOKENS, :]
    over_x = {"ty": (1 - xx) * 2 + core}
    over_y = {"tx": 1 - tx}
    over_c = {"ty": xx * 2 + (1 - core)}
    src_wa = (wq, wk, wv, wo)

    barrier = pltpu.get_barrier_semaphore()
    for peer in (over_x, over_y, over_c):
        pl.semaphore_signal(barrier, inc=1, device_id=peer, device_id_type=MESH)
    pl.semaphore_wait(barrier, 3)

    def remote(src, dst, send, recv, peer):
        return pltpu.make_async_remote_copy(src_ref=src, dst_ref=dst, send_sem=send, recv_sem=recv,
                                            device_id=peer, device_id_type=MESH)

    def own_ref(k):
        layer, kind, j = chunk_kind(k)
        if kind == "a":
            return src_wa[j].at[layer]
        if kind == "u":
            return wup.at[layer, :, j * UC:(j + 1) * UC]
        return wdown.at[layer, :, j * DC:(j + 1) * DC]

    def land_ref(k, s):
        layer, kind, j = chunk_kind(k)
        if kind == "a":
            return land_a.at[layer, s - 1, j * GF:(j + 1) * GF, :]
        if kind == "u":
            return land_u.at[layer, s - 1, :, j * UC:(j + 1) * UC]
        return land_d.at[layer, s - 1, :, j * DC:(j + 1) * DC]

    def weight_copy(k, s):
        if s == X:
            src, peer = own_ref(k), over_x
        elif s == Y:
            src, peer = own_ref(k), over_y
        elif s == C:
            src, peer = own_ref(k), over_c
        elif s == XY:
            src, peer = (land_ref(k, Y), over_x) if relay_on_x(k) else (land_ref(k, X), over_y)
        else:
            src, peer = land_ref(k, s - 1), over_c
        return remote(src, land_ref(k, s), wsend.at[k, s - 1], wrecv.at[k, s - 1], peer)

    def image_copy(i):
        theirs = (1 - tx) * 4 + ty
        return remote(x_in.at[theirs * IMGS + i], x1.at[i * NTOK:(i + 1) * NTOK, :], isend.at[i], irecv.at[i], over_y)

    def out_ref(s, q):
        cc, i = divmod(q, TILES)
        row, col = (s // 2) * TOKENS + i * TT, (s % 2) * HW + cc * DC
        return big.at[row:row + TT, col:col + DC]

    def out_copy(q, s):
        cc, i = divmod(q, TILES)
        if s == X:
            src, peer = out_ref(0, q), over_x
        elif s == C:
            src, peer = out_ref(0, q), over_c
        elif s == Y:
            src, peer = x1.at[i * TT:(i + 1) * TT, cc * DC:(cc + 1) * DC], over_y
        elif s == XY:
            src, peer = out_ref(Y, q), over_x
        else:
            src, peer = out_ref(s - 1, q), over_c
        return remote(src, out_ref(s, q), osend.at[q, s - 1], orecv.at[q, s - 1], peer)

    def out_arrived(q, s):
        return remote(out_ref(s, q), out_ref(s, q), osend.at[q, s - 1], orecv.at[q, s - 1], over_x)

    def small(src, dst, j, peer):
        return remote(src, dst, small_send.at[j], small_recv.at[j], peer)

    def vec_copy(j):
        return small(vec_own[j], vec_oth[j], j, over_y)

    def hid_copy(j, s):
        src = hid[j].at[X] if s == XC else hid_own[j]
        return small(src, hid[j].at[s], 6 + 3 * j + s - 1, over_x if s == X else over_c)

    def own_rows(i):
        return pltpu.make_async_copy(x_in.at[me * IMGS + i], big.at[i * NTOK:(i + 1) * NTOK, 0:HW], local_sem.at[i])

    def act(action):
        kind, *k = action
        k = k[0] if k else None
        if kind == "small":
            for j in range(3):
                hid_copy(j, X).start()
            for j in range(3):
                hid_copy(j, C).start()
            for j in range(6):
                vec_copy(j).start()
            for i in range(IMGS):
                own_rows(i).start()
        elif kind == "ownx":
            weight_copy(k, X).start()
        elif kind == "owny":
            weight_copy(k, Y).start()
        elif kind == "ownc":
            weight_copy(k, C).start()
        elif kind == "image":
            image_copy(k).start()
        elif kind == "gotx":
            weight_copy(k, X).wait_recv()
            weight_copy(k, XC).start()
        elif kind == "goty":
            weight_copy(k, Y).wait_recv()
            weight_copy(k, YC).start()
        elif kind == "relay":
            weight_copy(k, XY).start()
        elif kind == "gotd":
            weight_copy(k, XY).wait_recv()
            weight_copy(k, XYC).start()
        elif kind == "out":
            if k == 0:
                pl.semaphore_wait(credit, 3)
            for s in (X, C):
                out_copy(k, s).start()
        elif kind == "outp":
            out_copy(k, Y).start()
        elif kind == "leave":
            for peer in (over_x, over_y, over_c):
                pl.semaphore_signal(credit, inc=1, device_id=peer, device_id_type=MESH)
        elif kind == "outx":
            out_arrived(k, X).wait_recv()
            out_copy(k, XC).start()
        elif kind == "outy":
            out_arrived(k, Y).wait_recv()
            out_copy(k, XY).start()
            out_copy(k, YC).start()
        elif kind == "outd":
            out_arrived(k, XY).wait_recv()
            out_copy(k, XYC).start()
        elif kind == "la":
            layer, r = action[1:]
            for s in (r, 4 + r):
                if s % 2:
                    for j in range(3):
                        weight_copy(layer * PER_LAYER + j, s).wait_recv()
            start(a_loads(layer, r))
        elif kind == "lo":
            arrived(action[1] * PER_LAYER + 3)
            start(o_loads(action[1]))
        elif kind == "lu":
            arrived(action[1] * PER_LAYER + NA + action[2])
            start(u_loads(*action[1:]))
        elif kind == "ld":
            arrived(action[1] * PER_LAYER + NA + NU + action[2])
            start(d_loads(*action[1:]))

    def slot_ref(land, own, layer, s):
        return own.at[layer] if s == 0 else land.at[layer, s - 1]

    def a_loads(layer, r):
        out = []
        for dy in range(2):
            s = dy * 4 + r
            cols = slice(r * 2 * HW + dy * HW, r * 2 * HW + (dy + 1) * HW)
            if s == 0:
                for j in range(3):
                    out.append((src_wa[j].at[layer], u.at[j * GF:(j + 1) * GF, cols], asem.at[s, j]))
            else:
                out.append((land_a.at[layer, s - 1, 0:3 * GF, :], u.at[0:3 * GF, cols], asem.at[s, 0]))
        return [pltpu.make_async_copy(*c) for c in out]

    def o_loads(layer):
        out = []
        for r in range(4):
            for dy in range(2):
                s = dy * 4 + r
                src = wo.at[layer] if s == 0 else land_a.at[layer, s - 1, 3 * GF:4 * GF, :]
                at = 3 * GF + (r % 2) * GF
                cols = slice((r // 2) * 2 * HW + dy * HW, (r // 2) * 2 * HW + (dy + 1) * HW)
                out.append(pltpu.make_async_copy(src, u.at[at:at + GF, cols], asem.at[s, 3]))
        return out

    def u_loads(layer, k):
        b = k % 2
        out = []
        for r in range(4):
            for dy in range(2):
                s = dy * 4 + r
                src = slot_ref(land_u, wup, layer, s).at[:, k * UC:(k + 1) * UC]
                out.append(pltpu.make_async_copy(
                    src, big.at[(2 + b) * TOKENS + dy * HW:(2 + b) * TOKENS + (dy + 1) * HW, r * UC:(r + 1) * UC], usem.at[b, s]))
        return out

    def d_loads(layer, cc):
        b = cc % DB
        out = []
        for r in range(4):
            for dy in range(2):
                s = dy * 4 + r
                src = slot_ref(land_d, wdown, layer, s).at[:, cc * DC:(cc + 1) * DC]
                out.append(pltpu.make_async_copy(
                    src, dbuf.at[b, r * FB:(r + 1) * FB, dy * DC:(dy + 1) * DC], dsem.at[b, s]))
        return out

    def start(copies):
        for c in copies:
            c.start()

    def finish(copies):
        for c in copies:
            c.wait()

    def arrived(k):
        for s in (C, XC, YC, XYC):
            weight_copy(k, s).wait_recv()

    def vec_row(layer, j):
        return vec_own[j][layer:layer + 1, :], vec_oth[j][layer:layer + 1, :]

    def norm(layer, j, tile):
        g0, g1 = vec_row(layer, j)
        s0, s1 = vec_row(layer, j + 1)
        rows, group = 16, 8

        @pl.loop(0, TT // (rows * group))
        def _(i):
            ats = [pl.ds(pl.multiple_of(tile * TT + (i * group + m) * rows, rows), rows) for m in range(group)]
            pairs = [(x0[at, :].astype(F32), x1[at, :].astype(F32)) for at in ats]
            done = []
            for a, b in pairs:
                mean = jnp.sum(a + b, 1, keepdims=True) * (0.5 / HW)
                a = a - mean
                b = b - mean
                var = jnp.sum(a * a + b * b, 1, keepdims=True) * (0.5 / HW)
                inv = lax.rsqrt(var + EPS)
                done.append(((a * inv * g0 + s0).astype(BF16), (b * inv * g1 + s1).astype(BF16)))
            for at, (a, b) in zip(ats, done):
                h[at, :HW] = a
                h[at, HW:] = b

    scale = HD ** -0.5 * math.log2(math.e)

    def qkv_at(b, first, rows):
        return qkv.at[first:first + rows, :]

    def ones_rows():
        for hd in range(GH):
            qkv_at(0, 2 * GF + hd * VR + HD, 16)[...] = jnp.ones((16, TT), BF16)

    def column(ref, layer, r):
        rows = [jnp.broadcast_to(ref[r, layer, hd:hd + 1, :], (128, HD)).T for hd in range(GH)]
        col = jnp.concatenate(rows, 0)
        return jnp.concatenate([col] * (TT // 128), 1)

    def project_qkv(layer, n):
        r, tile, b = n // 4, lax.rem(n, 4), 0
        rows = pl.ds(pl.multiple_of(tile * TT, TT), TT)
        cols = pl.ds(pl.multiple_of(r * 2 * HW, 2 * HW), 2 * HW)
        t = dot(u[0:3 * GF, cols], h[rows, :], NT)
        qkv_at(b, 0, GF)[...] = (t[:GF] + column(hid[0], layer, r)).astype(BF16)
        qkv_at(b, GF, GF)[...] = t[GF:2 * GF].astype(BF16)
        t = (t[2 * GF:] + column(hid[1], layer, r)).astype(BF16)
        for hd in range(GH):
            qkv_at(b, 2 * GF + hd * VR, HD)[...] = t[hd * HD:(hd + 1) * HD, :]

    def heads(n):
        r, tile, b = n // 4, lax.rem(n, 4), 0
        score, weigh, value = [], [], []
        for img in range(TT // NTOK):
            c = slice(img * NTOK, (img + 1) * NTOK)
            for hd in range(GH):
                box = {}

                def f(hd=hd, c=c, box=box):
                    qt = qkv_at(b, hd * HD, HD)[:, c]
                    kt = qkv_at(b, GF + hd * HD, HD)[:, c]
                    box["s"] = dot(kt, qt, TN)

                def g(box=box):
                    st = box["s"]
                    box["e"] = jnp.exp2((st - jnp.max(st, 0, keepdims=True)) * scale).astype(BF16)

                def w(hd=hd, c=c, img=img, box=box):
                    t = dot(qkv_at(b, 2 * GF + hd * VR, VR)[:, c], box["e"])
                    at = pl.ds(pl.multiple_of(tile * 4 * GF + r * GF + hd * HD, 16), HD)
                    dbuf[img, at, :] = (t[:HD] * (1.0 / t[HD:HD + 1])).astype(BF16)
                score.append(f)
                weigh.append(g)
                value.append(w)
        return score, weigh, value

    def run_heads(n):
        score, weigh, value = heads(n)
        for f in score:
            f()
        for g, w in zip(weigh, value):
            g()
            w()

    def project_block(layer, tile):
        b0, b1 = vec_row(layer, 2)
        at = pl.ds(pl.multiple_of(tile * 4 * GF, 4 * GF), 4 * GF)
        o = jnp.concatenate([dbuf[img, at, :].T for img in range(TT // NTOK)], 0)
        rows = pl.ds(pl.multiple_of(tile * TT, TT), TT)
        for half, ref, bias in ((0, x0, b0), (1, x1, b1)):
            acc = dot(o[:, :HW], u[3 * GF:5 * GF, half * HW:(half + 1) * HW])
            acc += dot(o[:, HW:], u[3 * GF:5 * GF, 2 * HW + half * HW:2 * HW + (half + 1) * HW])
            ref[rows, :] = (ref[rows, :].astype(F32) + acc + bias).astype(BF16)

    def up_block(layer, k, tile, b):
        rows = pl.ds(pl.multiple_of(tile * TT, TT), TT)
        bias = jnp.concatenate(
            [hid[2][r, layer:layer + 1, pl.ds(pl.multiple_of(k * UC, 128), UC)] for r in range(4)], 1)
        for first in range(0, 4 * UC, NB):
            t = gelu(dot(h[rows, :], big[pl.ds(pl.multiple_of((2 + b) * TOKENS, TOKENS), 2 * HW), first:first + NB]) + bias[:, first:first + NB]).astype(BF16)
            at = first
            while at < first + NB:
                r, off = divmod(at, UC)
                size = min(UC - off, first + NB - at)
                u[rows, pl.ds(pl.multiple_of(r * FB + k * UC + off, 128), size)] = t[:, at - first:at - first + size]
                at += size

    def down_block(layer, cc, tile, b):
        rows = pl.ds(pl.multiple_of(tile * TT, TT), TT)
        cols = pl.ds(pl.multiple_of(cc * DC, DC), DC)
        acc = dot(u[rows, :], dbuf[b])
        for half, ref, vec in ((0, x0, vec_own[5]), (1, x1, vec_oth[5])):
            new = ref[rows, cols].astype(F32) + acc[:, half * DC:(half + 1) * DC] + vec[layer:layer + 1, cols]
            ref[rows, cols] = new.astype(BF16)

    program, _, _ = plan()
    before = {}
    todo = []
    tail = []
    for item in program:
        if item[0] == "do":
            todo.append(item[1])
        else:
            before[item[1:]] = todo
            todo = []
    tail = todo

    def ahead(layer, kind, n, first=0):
        def branch(some):
            if len(some) == 1:
                for a in before[(layer, kind, some[0])] if some[0] >= first else ():
                    act(a)
                return
            half = len(some) // 2

            @pl.when(n < some[half])
            def _():
                branch(some[:half])

            @pl.when(n >= some[half])
            def _():
                branch(some[half:])

        branch(range(BLOCKS[kind]))

    def straight(layer, kind, n):
        for a in before[(layer, kind, n)]:
            act(a)

    def at_loads(n, count, wait):
        for j in range(count):
            @pl.when(n == j * TILES)
            def _(j=j):
                finish(wait(j))

    def norm_first(layer, tile):
        if layer == 0:
            for i in range(2):
                image_copy(2 * tile + i).wait_recv()
        norm(layer, 0, tile)

    for layer in range(LAYERS):
        straight(layer, "a", 0)
        if layer == 0:
            for j in range(3):
                hid_copy(j, X).wait_recv()
                hid_copy(j, XC).start()
            for j in range(3):
                hid_copy(j, C).wait_recv()
                hid_copy(j, XC).wait_recv()
                hid[j][0] = hid_own[j][...]
            for j in range(6):
                vec_copy(j).wait_recv()
            for i in range(IMGS):
                own_rows(i).wait()
        ones_rows()

        @pl.loop(0, 4 * TILES)
        def _(n, layer=layer):
            ahead(layer, "a", n, 1)
            for r in range(4):
                @pl.when(n == 4 * r)
                def _(r=r):
                    finish(a_loads(layer, r))
            for tile in range(TILES):
                @pl.when(n == tile)
                def _(tile=tile):
                    norm_first(layer, tile)
            project_qkv(layer, n)

            @pl.when(n < BLOCKS["a"])
            def _():
                run_heads(n)

        @pl.loop(0, TILES)
        def _(n, layer=layer):
            ahead(layer, "p", n)

            @pl.when(n == 0)
            def _():
                finish(o_loads(layer))
            project_block(layer, n)
            norm(layer, 3, n)

        @pl.loop(0, NU * TILES)
        def _(n, layer=layer):
            ahead(layer, "u", n)
            k, tile = n // TILES, lax.rem(n, TILES)
            at_loads(n, NU, lambda j: u_loads(layer, j))
            up_block(layer, k, tile, lax.rem(k, 2))

        @pl.loop(0, ND * TILES)
        def _(n, layer=layer):
            ahead(layer, "d", n)
            cc, tile = n // TILES, lax.rem(n, TILES)
            at_loads(n, ND, lambda j: d_loads(layer, j))
            down_block(layer, cc, tile, lax.rem(cc, DB))

    for k in range(CHUNKS):
        for s in range(1, 8):
            weight_copy(k, s).wait_send()
    for i in range(IMGS):
        image_copy(i).wait_send()
    for j in range(6):
        vec_copy(j).wait_send()
    for j in range(3):
        for s in (X, C, XC):
            hid_copy(j, s).wait_send()
    def close(q):
        for s in (C, XC, YC, XYC):
            out_arrived(q, s).wait_recv()
        for s in range(1, 8):
            out_copy(q, s).wait_send()

    closed = 0
    for a in tail:
        act(a)
        if a[0] == "outd":
            while closed < a[1] - 3:
                close(closed)
                closed += 1
    for q in range(closed, UNITS):
        close(q)


def mega(x_in, wq, wk, wv, wo, wup, wdown, *small):
    any_spec = pl.BlockSpec(memory_space=pl.ANY)
    vm = pl.BlockSpec(memory_space=pltpu.VMEM)
    dma = pltpu.SemaphoreType.DMA
    shapes = ((LAYERS, 7, 4 * GF, HW), (LAYERS, 7, HW, FB), (LAYERS, 7, FB, HW))
    flops = 2 * TOKENS * FB * 16384 * LAYERS
    return pl.pallas_call(
        mega_kernel,
        out_shape=(pltpu.VMEM((4 * TOKENS, 2 * HW), BF16),) + tuple(jax.ShapeDtypeStruct(s, BF16) for s in shapes),
        in_specs=[any_spec] * 7 + [vm] * 9,
        out_specs=[vm] + [any_spec] * 3,
        scratch_shapes=[
            pltpu.VMEM((TOKENS, HW), BF16), pltpu.VMEM((TOKENS, 4 * FB), BF16),
            pltpu.VMEM((DB, 4 * FB, 2 * DC), BF16), pltpu.VMEM((2 * GF + GH * VR, TT), BF16),
            *[pltpu.VMEM(a.shape, F32) for a in small[:6]], *[pltpu.VMEM((4,) + a.shape, F32) for a in small[6:]],
            dma((CHUNKS, 7)), dma((CHUNKS, 7)), dma((IMGS,)), dma((IMGS,)), dma((UNITS, 7)), dma((UNITS, 7)),
            dma((15,)), dma((15,)), dma((IMGS,)), dma((8, 4)), dma((2, 8)), dma((DB, 8)), pltpu.SemaphoreType.REGULAR,
        ],
        compiler_params=pltpu.CompilerParams(collective_id=0, has_side_effects=True, vmem_limit_bytes=41000000),
        cost_estimate=pl.CostEstimate(flops=flops, bytes_accessed=300 << 20, transcendentals=0),
        name="encoder",
    )(x_in, wq, wk, wv, wo, wup, wdown, *small)[0]


def hand_over(big, shape):
    def copy(big_ref, out_ref, sems):
        me = lax.axis_index("tx") * 4 + lax.axis_index("ty")
        copies = []
        for s in range(8):
            place = sum(((me // bit + s // bit) % 2) * bit for bit in (1, 2, 4))
            for i in range(IMGS):
                row, col = (s // 2) * TOKENS + i * NTOK, (s % 2) * HW
                copies.append(pltpu.make_async_copy(
                    big_ref.at[row:row + NTOK, col:col + HW], out_ref.at[place * IMGS + i], sems.at[s, i]))
        for c in copies:
            c.start()
        for c in copies:
            c.wait()

    return pl.pallas_call(
        copy, out_shape=jax.ShapeDtypeStruct(shape, big.dtype),
        in_specs=[pl.BlockSpec(memory_space=pltpu.VMEM)], out_specs=pl.BlockSpec(memory_space=pl.ANY),
        scratch_shapes=[pltpu.SemaphoreType.DMA((8, IMGS))],
        compiler_params=pltpu.CompilerParams(vmem_limit_bytes=1 << 20), name="hand_over")(big)


def solution(mesh):
    act_spec = P("dp", None, "tx")
    vec_tx = P(None, "tx")
    proj_spec = P(None, "tx", "ty", None)
    head_vec = P(None, "ty", None)
    in_specs = (act_spec, vec_tx, vec_tx, proj_spec, head_vec, proj_spec, proj_spec, head_vec,
                P(None, "ty", None, "tx"), vec_tx, vec_tx, vec_tx,
                P(None, "tx", "ty"), P(None, "ty"), P(None, "ty", "tx"), vec_tx)

    def heads_first(w):
        return jnp.transpose(w, (0, 2, 3, 1)).reshape(LAYERS, GF, HW)

    def local_fn(x_in, ln1_gain, ln1_bias, w_q, b_q, w_k, w_v, b_v, w_o, b_o, ln2_gain, ln2_bias, w_up, b_up, w_down, b_down):
        big = mega(x_in, heads_first(w_q), heads_first(w_k), heads_first(w_v), w_o.reshape(LAYERS, GF, HW), w_up, w_down,
                   ln1_gain, ln1_bias, b_o, ln2_gain, ln2_bias, b_down, b_q, b_v, b_up)
        return hand_over(big, x_in.shape)

    return jax.shard_map(local_fn, mesh=mesh, in_specs=in_specs, out_specs=act_spec, check_vma=False)
```

time: 736 us -> 625 us (0.85)
  Pallas kernels: 707 us -> 625 us
  local copies, waits for them, and re-layouts: 27.1 us -> 0 us
    pallas_call x1 -> x2, Pallas kernels: 707 us -> 625 us  [the longest x1 616 us: mega(): pl.pallas_call(mega_kernel, out_shape=(pltpu.VMEM((4 * TOKENS, 2 * HW), B...]
    unnamed x6 -> x0, local copies, waits for them, and re-layouts: 24.2 us -> none
where the time goes in v2:
time: 625 us
  Pallas kernels  625 us (100%)
    pallas_call x1, Pallas kernels, mega(): pl.pallas_call(mega_kernel, out_shape=(pltpu.VMEM((4 * TOKENS, 2 * HW), B...  616 us

profile of v2, /device:TPU:0, one launch (start us, length us, event | category | flops | bytes accessed | tf_op | source)
XLA Modules:
  0.0 625.0 jit_solution(9080737138263586628)
XLA Ops:
  0.0 615.9 %encoder.1 = (bf16[8192,1536]{1,0:T(8,128)(2,1)S(1)}, bf16[2,7,1536,768]{3,2,1,0:T(8,128)(2,1)}, bf16[2,7,768,1536]{3,2,1,0:T(8,128)(2,1)}, bf16[2,7,1536,768]{3,2,1,0:T(8,128)(2,1)}) custom-call(bf16[64,256,768]{2,1,0:T(8,128)(2,1)} %x_in.1, bf16[2,384,768]{2,1,0:T(8,128)(2,1)} %bitcast.10, bf16[2,384,768]{2,1,0:T(8,128)(2,1)} %bitcast.11, ...), custom_call_target="tpu_custom_call" | custom-call | flops 206158430208 | bytes 314572800 | tf_op jit(solution)/shard_map/encoder/pallas_call | solution.py:710
  615.9 8.9 %hand_over.1 = bf16[64,256,768]{2,1,0:T(8,128)(2,1)} custom-call(bf16[8192,1536]{1,0:T(8,128)(2,1)S(1)} %get-tuple-element.6.big_ref), custom_call_target="tpu_custom_call" | custom-call | tf_op jit(solution)/shard_map/hand_over/pallas_call | solution.py:743

commit v3 on v2

--- a/solution.py
+++ b/solution.py
@@ -61,12 +61,12 @@
 
 LINK = 46.6e3
 BACKLOG = 12.0
-MODES = "xxxxxyxxyxxxyxxyyyyxyxyyyyyy"
-RANK_X = "fhihkapyflvgprzumqtwuwsxzzzu"
-RANK_Y = "hlbjoqorrtnphopfjmmonfkjiljh"
-RANK_R = "cxtlosbypmfyjtepgfjseseimaah"
-RANK_I = "coboceni"
-EARLY, OUTS = 17, 2
+MODES = "xxyxxxxxxyyxxxxyyyxyyxyyyyyy"
+RANK_X = "qqqqddddiiiiiiccccnnnnjjjjjj"
+RANK_Y = "ttttssssllllllqqqqssssqqqqqq"
+RANK_R = "qqqqrrrraaaaaammmmffffrrrrrr"
+RANK_I = "wjlqemul"
+EARLY, OUTS = -20, 2
 BLOCKS = {"a": 16, "p": TILES, "u": NU * TILES, "d": ND * TILES}
 
 
@@ -220,9 +220,8 @@
                 do(("leave",))
             block(layer, "d", n, [("ld", layer, n // TILES)], block_cost("d", n))
             mark.append(now[0])
-            if layer == LAYERS - 1 and n >= 1:
-                do(("out", n - 1))
-    do(("out", UNITS - 1))
+            if layer == LAYERS - 1:
+                do(("out", n))
     while pending or queue["y"]:
         times = [p[0] for p in pending] + [free["y"] - BACKLOG + 1e-6 for _ in queue["y"]]
         now[0] = max(now[0], min(times))
@@ -240,7 +239,7 @@
 
 def encoder_body(x_in, wq, wk, wv, wo, wup, wdown, vec_own, hid_own, big, land_a, land_u, land_d,
                  x1, u, dbuf, qkv, vec_oth, hid,
-                wsend, wrecv, isend, irecv, osend, orecv, small_send, small_recv,
+                wsend, wrecv, arecv, crecv, isend, irecv, osend, orecv, small_send, small_recv,
                 local_sem, asem, usem, dsem, credit):
     ty, tx = lax.axis_index("ty"), lax.axis_index("tx")
     core, xx = lax.rem(ty, 2), ty // 2
@@ -288,11 +287,23 @@
             src, peer = (land_ref(k, Y), over_x) if relay_on_x(k) else (land_ref(k, X), over_y)
         else:
             src, peer = land_ref(k, s - 1), over_c
-        return remote(src, land_ref(k, s), wsend.at[k, s - 1], wrecv.at[k, s - 1], peer)
+        return remote(src, land_ref(k, s), wsend.at[s - 1], landed(k, s), peer)
+
+    def landed(k, s):
+        layer, kind, j = chunk_kind(k)
+        hop = (X, Y, XY).index(s) if s in (X, Y, XY) else 3
+        if kind != "a":
+            return wrecv.at[k - (layer + 1) * NA, hop]
+        if hop < 3:
+            return arecv.at[layer * NA + j, hop]
+        return crecv.at[layer, 4 if j == 3 else s // 2]
+
+    def whole(ref, sem):
+        return remote(ref, ref, wsend.at[0], sem, over_c).wait_recv()
 
     def image_copy(i):
         theirs = (1 - tx) * 4 + ty
-        return remote(x_in.at[theirs * IMGS + i], x1.at[i * NTOK:(i + 1) * NTOK, :], isend.at[i], irecv.at[i], over_y)
+        return remote(x_in.at[theirs * IMGS + i], x1.at[i * NTOK:(i + 1) * NTOK, :], isend.at[0], irecv.at[i // 2], over_y)
 
     def out_ref(s, q):
         cc, i = divmod(q, TILES)
@@ -311,10 +322,13 @@
             src, peer = out_ref(Y, q), over_x
         else:
             src, peer = out_ref(s - 1, q), over_c
-        return remote(src, out_ref(s, q), osend.at[q, s - 1], orecv.at[q, s - 1], peer)
+        return remote(src, out_ref(s, q), osend.at[s - 1], left(q, s), peer)
+
+    def left(q, s):
+        return orecv.at[q, (X, Y, XY).index(s)] if s in (X, Y, XY) else osend.at[7]
 
     def out_arrived(q, s):
-        return remote(out_ref(s, q), out_ref(s, q), osend.at[q, s - 1], orecv.at[q, s - 1], over_x)
+        return remote(out_ref(s, q), out_ref(s, q), osend.at[s - 1], left(q, s), over_x)
 
     def small(src, dst, j, peer):
         return remote(src, dst, small_send.at[j], small_recv.at[j], peer)
@@ -327,7 +341,7 @@
         return small(src, hid[j].at[s], 6 + 3 * j + s - 1, over_x if s == X else over_c)
 
     def own_rows(i):
-        return pltpu.make_async_copy(x_in.at[me * IMGS + i], big.at[i * NTOK:(i + 1) * NTOK, 0:HW], local_sem.at[i])
+        return pltpu.make_async_copy(x_in.at[me * IMGS + i], big.at[i * NTOK:(i + 1) * NTOK, 0:HW], local_sem.at[0])
 
     def act(action):
         kind, *k = action
@@ -384,8 +398,7 @@
             layer, r = action[1:]
             for s in (r, 4 + r):
                 if s % 2:
-                    for j in range(3):
-                        weight_copy(layer * PER_LAYER + j, s).wait_recv()
+                    whole(land_a.at[layer, s - 1, 0:3 * GF, :], crecv.at[layer, s // 2])
             start(a_loads(layer, r))
         elif kind == "lo":
             arrived(action[1] * PER_LAYER + 3)
@@ -407,9 +420,9 @@
             cols = slice(r * 2 * HW + dy * HW, r * 2 * HW + (dy + 1) * HW)
             if s == 0:
                 for j in range(3):
-                    out.append((src_wa[j].at[layer], u.at[j * GF:(j + 1) * GF, cols], asem.at[s, j]))
+                    out.append((src_wa[j].at[layer], u.at[j * GF:(j + 1) * GF, cols], asem.at[r]))
             else:
-                out.append((land_a.at[layer, s - 1, 0:3 * GF, :], u.at[0:3 * GF, cols], asem.at[s, 0]))
+                out.append((land_a.at[layer, s - 1, 0:3 * GF, :], u.at[0:3 * GF, cols], asem.at[r]))
         return [pltpu.make_async_copy(*c) for c in out]
 
     def o_loads(layer):
@@ -420,7 +433,7 @@
                 src = wo.at[layer] if s == 0 else land_a.at[layer, s - 1, 3 * GF:4 * GF, :]
                 at = 3 * GF + (r % 2) * GF
                 cols = slice((r // 2) * 2 * HW + dy * HW, (r // 2) * 2 * HW + (dy + 1) * HW)
-                out.append(pltpu.make_async_copy(src, u.at[at:at + GF, cols], asem.at[s, 3]))
+                out.append(pltpu.make_async_copy(src, u.at[at:at + GF, cols], asem.at[4]))
         return out
 
     def u_loads(layer, k):
@@ -431,7 +444,7 @@
                 s = dy * 4 + r
                 src = slot_ref(land_u, wup, layer, s).at[:, k * UC:(k + 1) * UC]
                 out.append(pltpu.make_async_copy(
-                    src, big.at[(2 + b) * TOKENS + dy * HW:(2 + b) * TOKENS + (dy + 1) * HW, r * UC:(r + 1) * UC], usem.at[b, s]))
+                    src, big.at[(2 + b) * TOKENS + dy * HW:(2 + b) * TOKENS + (dy + 1) * HW, r * UC:(r + 1) * UC], usem.at[b]))
         return out
 
     def d_loads(layer, cc):
@@ -442,20 +455,38 @@
                 s = dy * 4 + r
                 src = slot_ref(land_d, wdown, layer, s).at[:, cc * DC:(cc + 1) * DC]
                 out.append(pltpu.make_async_copy(
-                    src, dbuf.at[b, r * FB:(r + 1) * FB, dy * DC:(dy + 1) * DC], dsem.at[b, s]))
+                    src, dbuf.at[b, r * FB:(r + 1) * FB, dy * DC:(dy + 1) * DC], dsem.at[b]))
         return out
 
     def start(copies):
         for c in copies:
             c.start()
 
-    def finish(copies):
-        for c in copies:
-            c.wait()
+    def loaded(ref, sem):
+        pltpu.make_async_copy(ref, ref, sem).wait()
+
+    def a_loaded(r):
+        loaded(u.at[0:3 * GF, r * 2 * HW:(r + 1) * 2 * HW], asem.at[r])
+
+    def o_loaded():
+        loaded(u.at[3 * GF:5 * GF, 0:4 * HW], asem.at[4])
+
+    def u_loaded(k):
+        at = (2 + k % 2) * TOKENS
+        loaded(big.at[at:at + 2 * HW, :], usem.at[k % 2])
+
+    def d_loaded(cc):
+        loaded(dbuf.at[cc % DB], dsem.at[cc % DB])
 
     def arrived(k):
-        for s in (C, XC, YC, XYC):
-            weight_copy(k, s).wait_recv()
+        layer, kind, j = chunk_kind(k)
+        if kind == "a":
+            ref = land_a.at[layer, 0:4, j * GF:(j + 1) * GF, :]
+        elif kind == "u":
+            ref = land_u.at[layer, 0:4, :, j * UC:(j + 1) * UC]
+        else:
+            ref = land_d.at[layer, 0:4, :, j * DC:(j + 1) * DC]
+        whole(ref, landed(k, C))
 
     def vec_row(layer, j):
         return vec_own[j][layer:layer + 1, :], vec_oth[j][layer:layer + 1, :]
@@ -609,12 +640,11 @@
         for j in range(count):
             @pl.when(n == j * TILES)
             def _(j=j):
-                finish(wait(j))
+                wait(j)
 
     def norm_first(layer, tile):
         if layer == 0:
-            for i in range(2):
-                image_copy(2 * tile + i).wait_recv()
+            whole(x1.at[tile * TT:(tile + 1) * TT, :], irecv.at[tile])
         norm(layer, 0, tile)
 
     for layer in range(LAYERS):
@@ -629,8 +659,7 @@
                 hid[j][0] = hid_own[j][...]
             for j in range(6):
                 vec_copy(j).wait_recv()
-            for i in range(IMGS):
-                own_rows(i).wait()
+            loaded(x0, local_sem.at[0])
         ones_rows()
 
         @pl.loop(0, 4 * TILES)
@@ -639,7 +668,7 @@
             for r in range(4):
                 @pl.when(n == 4 * r)
                 def _(r=r):
-                    finish(a_loads(layer, r))
+                    a_loaded(r)
             for tile in range(TILES):
                 @pl.when(n == tile)
                 def _(tile=tile):
@@ -656,7 +685,7 @@
 
             @pl.when(n == 0)
             def _():
-                finish(o_loads(layer))
+                o_loaded()
             project_block(layer, n)
             norm(layer, 3, n)
 
@@ -664,41 +693,32 @@
         def _(n, layer=layer):
             ahead(layer, "u", n)
             k, tile = n // TILES, lax.rem(n, TILES)
-            at_loads(n, NU, lambda j: u_loads(layer, j))
+            at_loads(n, NU, u_loaded)
             up_block(layer, k, tile, lax.rem(k, 2))
 
         @pl.loop(0, ND * TILES)
         def _(n, layer=layer):
             ahead(layer, "d", n)
             cc, tile = n // TILES, lax.rem(n, TILES)
-            at_loads(n, ND, lambda j: d_loads(layer, j))
+            at_loads(n, ND, d_loaded)
             down_block(layer, cc, tile, lax.rem(cc, DB))
 
-    for k in range(CHUNKS):
-        for s in range(1, 8):
-            weight_copy(k, s).wait_send()
-    for i in range(IMGS):
-        image_copy(i).wait_send()
+    def sent(ref, sem):
+        remote(ref, ref, sem, irecv.at[0], over_c).wait_send()
+
+    for s in range(7):
+        sent(land_a.at[0, 0:6], wsend.at[s])
+    sent(x1, isend.at[0])
     for j in range(6):
         vec_copy(j).wait_send()
     for j in range(3):
         for s in (X, C, XC):
             hid_copy(j, s).wait_send()
-    def close(q):
-        for s in (C, XC, YC, XYC):
-            out_arrived(q, s).wait_recv()
-        for s in range(1, 8):
-            out_copy(q, s).wait_send()
-
-    closed = 0
     for a in tail:
         act(a)
-        if a[0] == "outd":
-            while closed < a[1] - 3:
-                close(closed)
-                closed += 1
-    for q in range(closed, UNITS):
-        close(q)
+    whole(big.at[0:2 * TOKENS, :], osend.at[7])
+    for s in range(7):
+        sent(x1, osend.at[s])
 
 
 def mega(x_in, wq, wk, wv, wo, wup, wdown, *small):
@@ -716,8 +736,9 @@
             pltpu.VMEM((TOKENS, HW), BF16), pltpu.VMEM((TOKENS, 4 * FB), BF16),
             pltpu.VMEM((DB, 4 * FB, 2 * DC), BF16), pltpu.VMEM((2 * GF + GH * VR, TT), BF16),
             *[pltpu.VMEM(a.shape, F32) for a in small[:6]], *[pltpu.VMEM((4,) + a.shape, F32) for a in small[6:]],
-            dma((CHUNKS, 7)), dma((CHUNKS, 7)), dma((IMGS,)), dma((IMGS,)), dma((UNITS, 7)), dma((UNITS, 7)),
-            dma((15,)), dma((15,)), dma((IMGS,)), dma((8, 4)), dma((2, 8)), dma((DB, 8)), pltpu.SemaphoreType.REGULAR,
+            dma((7,)), dma((LAYERS * (NU + ND), 4)), dma((LAYERS * NA, 3)), dma((LAYERS, 5)),
+            dma((1,)), dma((TILES,)), dma((8,)), dma((UNITS, 3)),
+            dma((15,)), dma((15,)), dma((1,)), dma((5,)), dma((2,)), dma((DB,)), pltpu.SemaphoreType.REGULAR,
         ],
         compiler_params=pltpu.CompilerParams(collective_id=0, has_side_effects=True, vmem_limit_bytes=41000000),
         cost_estimate=pl.CostEstimate(flops=flops, bytes_accessed=300 << 20, transcendentals=0),
@@ -726,7 +747,7 @@
 
 
 def hand_over(big, shape):
-    def copy(big_ref, out_ref, sems):
+    def copy(big_ref, out_ref, sem):
         me = lax.axis_index("tx") * 4 + lax.axis_index("ty")
         copies = []
         for s in range(8):
@@ -734,16 +755,15 @@
             for i in range(IMGS):
                 row, col = (s // 2) * TOKENS + i * NTOK, (s % 2) * HW
                 copies.append(pltpu.make_async_copy(
-                    big_ref.at[row:row + NTOK, col:col + HW], out_ref.at[place * IMGS + i], sems.at[s, i]))
+                    big_ref.at[row:row + NTOK, col:col + HW], out_ref.at[place * IMGS + i], sem))
         for c in copies:
             c.start()
-        for c in copies:
-            c.wait()
+        pltpu.make_async_copy(out_ref, out_ref, sem).wait()
 
     return pl.pallas_call(
         copy, out_shape=jax.ShapeDtypeStruct(shape, big.dtype),
         in_specs=[pl.BlockSpec(memory_space=pltpu.VMEM)], out_specs=pl.BlockSpec(memory_space=pl.ANY),
-        scratch_shapes=[pltpu.SemaphoreType.DMA((8, IMGS))],
+        scratch_shapes=[pltpu.SemaphoreType.DMA],
         compiler_params=pltpu.CompilerParams(vmem_limit_bytes=1 << 20), name="hand_over")(big)
 
 

time: 625 us -> 617 us (0.987)
  Pallas kernels: 625 us -> 616 us
    pallas_call x1, Pallas kernels: 616 us -> 608 us  [mega(): pl.pallas_call(mega_kernel, out_shape=(pltpu.VMEM((4 * TOKENS, 2 * HW), B...]
where the time goes in v3:
time: 617 us
  Pallas kernels  616 us (100%)
    pallas_call x1, Pallas kernels, mega(): pl.pallas_call(mega_kernel, out_shape=(pltpu.VMEM((4 * TOKENS, 2 * HW), B...  608 us

profile of v3, /device:TPU:0, one launch (start us, length us, event | category | flops | bytes accessed | tf_op | source)
XLA Modules:
  0.0 616.5 jit_solution(1174216610997107412)
XLA Ops:
  0.0 608.0 %encoder.1 = (bf16[8192,1536]{1,0:T(8,128)(2,1)S(1)}, bf16[2,7,1536,768]{3,2,1,0:T(8,128)(2,1)}, bf16[2,7,768,1536]{3,2,1,0:T(8,128)(2,1)}, bf16[2,7,1536,768]{3,2,1,0:T(8,128)(2,1)}) custom-call(bf16[64,256,768]{2,1,0:T(8,128)(2,1)} %x_in.1, bf16[2,384,768]{2,1,0:T(8,128)(2,1)} %bitcast.10, bf16[2,384,768]{2,1,0:T(8,128)(2,1)} %bitcast.11, ...), custom_call_target="tpu_custom_call" | custom-call | flops 206158430208 | bytes 314572800 | tf_op jit(solution)/shard_map/encoder/pallas_call | solution.py:730
  608.0 8.3 %hand_over.1 = bf16[64,256,768]{2,1,0:T(8,128)(2,1)} custom-call(bf16[8192,1536]{1,0:T(8,128)(2,1)S(1)} %get-tuple-element.6.big_ref), custom_call_target="tpu_custom_call" | custom-call | tf_op jit(solution)/shard_map/hand_over/pallas_call | solution.py:763

commit v4 on v3

--- a/solution.py
+++ b/solution.py
@@ -61,12 +61,13 @@
 
 LINK = 46.6e3
 BACKLOG = 12.0
-MODES = "xxyxxxxxxyyxxxxyyyxyyxyyyyyy"
-RANK_X = "qqqqddddiiiiiiccccnnnnjjjjjj"
-RANK_Y = "ttttssssllllllqqqqssssqqqqqq"
-RANK_R = "qqqqrrrraaaaaammmmffffrrrrrr"
-RANK_I = "wjlqemul"
-EARLY, OUTS = -20, 2
+MODES = "yxxyxxxxxxyxxxyyyxxyyxyyyyyy"
+RANK_X = "uuruyvywnqtqqskjnmuqoonqomqo"
+RANK_Y = "gjhgpqqoiiiighdedgecaenonmkl"
+RANK_R = "oqpmsvvtqooqssgieilnoqnlnlln"
+RANK_I = "ntkhrrlh"
+EARLY, OUTS = -17, 4
+AROUND = 3
 BLOCKS = {"a": 16, "p": TILES, "u": NU * TILES, "d": ND * TILES}
 
 
@@ -120,10 +121,12 @@
         loads.append((("lo", layer), [("w", s, base + 3) for s in range(1, 8)], old, 2.2))
         for k in range(NU):
             last = (layer, "u", (k - 2) * TILES + TILES - 1) if k > 1 else old and (layer - 1, "u", BLOCKS["u"] - 1)
-            loads.append((("lu", layer, k), [("w", s, base + NA + k) for s in range(1, 8)], last, 2.2))
+            loads.append((("lu", layer, k), [("w", s, base + NA + k) for s in range(1, 6)], last, 1.8))
+            loads.append((("mu", layer, k), [("w", s, base + NA + k) for s in (XY, XYC)], last, 1.1))
         for j in range(ND):
             last = (layer, "d", (j - DB) * TILES + TILES - 1) if j >= DB else (layer, "p", TILES - 1)
-            loads.append((("ld", layer, j), [("w", s, base + NA + NU + j) for s in range(1, 8)], last, 1.8))
+            loads.append((("ld", layer, j), [("w", s, base + NA + NU + j) for s in range(1, 6)], last, 1.5))
+            loads.append((("md", layer, j), [("w", s, base + NA + NU + j) for s in (XY, XYC)], last, 1.0))
 
     def do(action):
         program.append(("do", action))
@@ -153,12 +156,19 @@
             queue["y"].append((10 * CHUNKS - EARLY + OUTS * k, ("outp", k)))
             arrive(("o", X, k), send("x", unit), ("outx", k))
             arrive(("o", C, k), send("c", unit))
+            if k < AROUND:
+                arrive(("z", k), send("x", unit), ("pass", k))
+        elif kind == "pass":
+            queue["y"].append((20 * CHUNKS + k, ("passy", k)))
+        elif kind == "passy":
+            arrive(("o", XY, k), send("y", unit), ("outd", k))
         elif kind == "outp":
             arrive(("o", Y, k), send("y", unit), ("outy", k))
         elif kind == "outx":
             arrive(("o", XC, k), send("c", unit))
         elif kind == "outy":
-            arrive(("o", XY, k), send("x", unit), ("outd", k))
+            if k >= AROUND:
+                arrive(("o", XY, k), send("x", unit), ("outd", k))
             arrive(("o", YC, k), send("c", unit))
         elif kind == "outd":
             arrive(("o", XYC, k), send("c", unit))
@@ -214,11 +224,11 @@
         for n in range(TILES):
             block(layer, "p", n, [("lo", layer)], block_cost("p", n))
         for n in range(BLOCKS["u"]):
-            block(layer, "u", n, [("lu", layer, n // TILES)], block_cost("u", n))
+            block(layer, "u", n, [("lu", layer, n // TILES), ("mu", layer, n // TILES)], block_cost("u", n))
         for n in range(BLOCKS["d"]):
             if layer == LAYERS - 1 and n == 0:
                 do(("leave",))
-            block(layer, "d", n, [("ld", layer, n // TILES)], block_cost("d", n))
+            block(layer, "d", n, [("ld", layer, n // TILES), ("md", layer, n // TILES)], block_cost("d", n))
             mark.append(now[0])
             if layer == LAYERS - 1:
                 do(("out", n))
@@ -240,7 +250,7 @@
 def encoder_body(x_in, wq, wk, wv, wo, wup, wdown, vec_own, hid_own, big, land_a, land_u, land_d,
                  x1, u, dbuf, qkv, vec_oth, hid,
                 wsend, wrecv, arecv, crecv, isend, irecv, osend, orecv, small_send, small_recv,
-                local_sem, asem, usem, dsem, credit):
+                local_sem, asem, usem, dsem, zsend, zrecv, credit):
     ty, tx = lax.axis_index("ty"), lax.axis_index("tx")
     core, xx = lax.rem(ty, 2), ty // 2
     me = tx * 4 + ty
@@ -291,7 +301,7 @@
 
     def landed(k, s):
         layer, kind, j = chunk_kind(k)
-        hop = (X, Y, XY).index(s) if s in (X, Y, XY) else 3
+        hop = (X, Y, XY).index(s) if s in (X, Y, XY) else 4 if s == XYC and kind != "a" else 3
         if kind != "a":
             return wrecv.at[k - (layer + 1) * NA, hop]
         if hop < 3:
@@ -309,6 +319,14 @@
         cc, i = divmod(q, TILES)
         row, col = (s // 2) * TOKENS + i * TT, (s % 2) * HW + cc * DC
         return big.at[row:row + TT, col:col + DC]
+
+    def aside(q):
+        return qkv.at[q // 4 * TT:(q // 4 + 1) * TT, q % 4 * DC:(q % 4 + 1) * DC]
+
+    def aside_copy(q):
+        cc, i = divmod(q, TILES)
+        src = x1.at[i * TT:(i + 1) * TT, cc * DC:(cc + 1) * DC]
+        return remote(src, aside(q), zsend.at[q], zrecv.at[q], over_x)
 
     def out_copy(q, s):
         cc, i = divmod(q, TILES)
@@ -319,7 +337,7 @@
         elif s == Y:
             src, peer = x1.at[i * TT:(i + 1) * TT, cc * DC:(cc + 1) * DC], over_y
         elif s == XY:
-            src, peer = out_ref(Y, q), over_x
+            src, peer = (aside(q), over_y) if q < AROUND else (out_ref(Y, q), over_x)
         else:
             src, peer = out_ref(s - 1, q), over_c
         return remote(src, out_ref(s, q), osend.at[s - 1], left(q, s), peer)
@@ -379,6 +397,12 @@
                 pl.semaphore_wait(credit, 3)
             for s in (X, C):
                 out_copy(k, s).start()
+            if k < AROUND:
+                aside_copy(k).start()
+        elif kind == "pass":
+            aside_copy(k).wait_recv()
+        elif kind == "passy":
+            out_copy(k, XY).start()
         elif kind == "outp":
             out_copy(k, Y).start()
         elif kind == "leave":
@@ -389,7 +413,8 @@
             out_copy(k, XC).start()
         elif kind == "outy":
             out_arrived(k, Y).wait_recv()
-            out_copy(k, XY).start()
+            if k >= AROUND:
+                out_copy(k, XY).start()
             out_copy(k, YC).start()
         elif kind == "outd":
             out_arrived(k, XY).wait_recv()
@@ -405,10 +430,16 @@
             start(o_loads(action[1]))
         elif kind == "lu":
             arrived(action[1] * PER_LAYER + NA + action[2])
-            start(u_loads(*action[1:]))
+            start(u_loads(*action[1:])[:6])
         elif kind == "ld":
             arrived(action[1] * PER_LAYER + NA + NU + action[2])
-            start(d_loads(*action[1:]))
+            start(d_loads(*action[1:])[:6])
+        elif kind == "mu":
+            weight_copy(action[1] * PER_LAYER + NA + action[2], XYC).wait_recv()
+            start(u_loads(*action[1:])[6:])
+        elif kind == "md":
+            weight_copy(action[1] * PER_LAYER + NA + NU + action[2], XYC).wait_recv()
+            start(d_loads(*action[1:])[6:])
 
     def slot_ref(land, own, layer, s):
         return own.at[layer] if s == 0 else land.at[layer, s - 1]
@@ -439,8 +470,8 @@
     def u_loads(layer, k):
         b = k % 2
         out = []
-        for r in range(4):
-            for dy in range(2):
+        for dy in range(2):
+            for r in range(4):
                 s = dy * 4 + r
                 src = slot_ref(land_u, wup, layer, s).at[:, k * UC:(k + 1) * UC]
                 out.append(pltpu.make_async_copy(
@@ -450,8 +481,8 @@
     def d_loads(layer, cc):
         b = cc % DB
         out = []
-        for r in range(4):
-            for dy in range(2):
+        for dy in range(2):
+            for r in range(4):
                 s = dy * 4 + r
                 src = slot_ref(land_d, wdown, layer, s).at[:, cc * DC:(cc + 1) * DC]
                 out.append(pltpu.make_async_copy(
@@ -483,9 +514,9 @@
         if kind == "a":
             ref = land_a.at[layer, 0:4, j * GF:(j + 1) * GF, :]
         elif kind == "u":
-            ref = land_u.at[layer, 0:4, :, j * UC:(j + 1) * UC]
+            ref = land_u.at[layer, 0:3, :, j * UC:(j + 1) * UC]
         else:
-            ref = land_d.at[layer, 0:4, :, j * DC:(j + 1) * DC]
+            ref = land_d.at[layer, 0:3, :, j * DC:(j + 1) * DC]
         whole(ref, landed(k, C))
 
     def vec_row(layer, j):
@@ -716,6 +747,8 @@
             hid_copy(j, s).wait_send()
     for a in tail:
         act(a)
+    for q in range(AROUND):
+        aside_copy(q).wait_send()
     whole(big.at[0:2 * TOKENS, :], osend.at[7])
     for s in range(7):
         sent(x1, osend.at[s])
@@ -736,9 +769,9 @@
             pltpu.VMEM((TOKENS, HW), BF16), pltpu.VMEM((TOKENS, 4 * FB), BF16),
             pltpu.VMEM((DB, 4 * FB, 2 * DC), BF16), pltpu.VMEM((2 * GF + GH * VR, TT), BF16),
             *[pltpu.VMEM(a.shape, F32) for a in small[:6]], *[pltpu.VMEM((4,) + a.shape, F32) for a in small[6:]],
-            dma((7,)), dma((LAYERS * (NU + ND), 4)), dma((LAYERS * NA, 3)), dma((LAYERS, 5)),
+            dma((7,)), dma((LAYERS * (NU + ND), 5)), dma((LAYERS * NA, 3)), dma((LAYERS, 5)),
             dma((1,)), dma((TILES,)), dma((8,)), dma((UNITS, 3)),
-            dma((15,)), dma((15,)), dma((1,)), dma((5,)), dma((2,)), dma((DB,)), pltpu.SemaphoreType.REGULAR,
+            dma((15,)), dma((15,)), dma((1,)), dma((5,)), dma((2,)), dma((DB,)), dma((AROUND,)), dma((AROUND,)), pltpu.SemaphoreType.REGULAR,
         ],
         compiler_params=pltpu.CompilerParams(collective_id=0, has_side_effects=True, vmem_limit_bytes=41000000),
         cost_estimate=pl.CostEstimate(flops=flops, bytes_accessed=300 << 20, transcendentals=0),

time: 617 us -> 615 us (level)
  no operation moved by 1% of the time
where the time goes in v4:
time: 615 us; the launch traced here: 614 us
  Pallas kernels  614 us (100%)
    pallas_call x1, Pallas kernels, mega(): pl.pallas_call(mega_kernel, out_shape=(pltpu.VMEM((4 * TOKENS, 2 * HW), B...  606 us

profile of v4, /device:TPU:0, one launch (start us, length us, event | category | flops | bytes accessed | tf_op | source)
XLA Modules:
  0.0 614.4 jit_solution(17859579945158184149)
XLA Ops:
  0.0 605.9 %encoder.1 = (bf16[8192,1536]{1,0:T(8,128)(2,1)S(1)}, bf16[2,7,1536,768]{3,2,1,0:T(8,128)(2,1)}, bf16[2,7,768,1536]{3,2,1,0:T(8,128)(2,1)}, bf16[2,7,1536,768]{3,2,1,0:T(8,128)(2,1)}) custom-call(bf16[64,256,768]{2,1,0:T(8,128)(2,1)} %x_in.1, bf16[2,384,768]{2,1,0:T(8,128)(2,1)} %bitcast.10, bf16[2,384,768]{2,1,0:T(8,128)(2,1)} %bitcast.11, ...), custom_call_target="tpu_custom_call" | custom-call | flops 206158430208 | bytes 314572800 | tf_op jit(solution)/shard_map/encoder/pallas_call | solution.py:763
  605.9 8.3 %hand_over.1 = bf16[64,256,768]{2,1,0:T(8,128)(2,1)} custom-call(bf16[8192,1536]{1,0:T(8,128)(2,1)S(1)} %get-tuple-element.6.big_ref), custom_call_target="tpu_custom_call" | custom-call | tf_op jit(solution)/shard_map/hand_over/pallas_call | solution.py:796
